TPU v7x, 32 devices: a whole 2x2x4 slice. The times are simulated.
32 devices in a mesh: groups: 2 (over x), mp: 16 (over z, y, core).
Axes of the slice: x: 2, y: 2, z: 4, core: 2. Of those that a mesh axis runs over, the one named last changes fastest.
Arguments:
- hidden: bfloat16 [1024, 4096], P(('groups', 'mp')), parts along dimension 0, may hold values from -6 to 6
- norm_gain_attn: float32 [4096], replicated, may hold values from 0.5 to 1.5
- w_query: bfloat16 [4096, 1024], P(None, 'mp'), may hold values from -0.09375 to 0.09375
- entering_kv: bfloat16 [16, 2048, 2048], P('groups', 'mp'), parts along dimension 0, may hold values from -60 to 60
- cached_kv: bfloat16 [16, 2048, 2048], P('groups', None, 'mp'), parts along dimension 0, may hold values from -60 to 60
- enc_lengths: int32 [2, 16], P(None, 'groups'), parts along dimension 1, may hold values from 128 to 2048
- w_out: bfloat16 [1024, 4096], P('mp'), may hold values from -0.1875 to 0.1875
- norm_gain_ffn: float32 [4096], replicated, may hold values from 0.5 to 1.5
- w_gate: bfloat16 [4096, 10240], P(None, 'mp'), may hold values from -0.09375 to 0.09375
- w_up: bfloat16 [4096, 10240], P(None, 'mp'), may hold values from -0.09375 to 0.09375
- w_down: bfloat16 [10240, 4096], P('mp'), may hold values from -0.0625 to 0.0625
Outputs:
- output: bfloat16 [1024, 4096], P(('groups', 'mp')), parts along dimension 0
There are 2 independent parts, one for each index of `groups`. A program takes and returns all parts, laid end to end along the dimension named above; an argument that names none is the same for every part. Nothing has to cross between parts.
All inputs are finite; a program needn't handle non-finite values.
Results may differ from a plain program's by a relative error of at most 0.0095.
The roundings to bfloat16 on the way count: a program that leaves them out, or rounds other values in their place, can miss the bound.
Values may be sent and summed in bfloat16 or wider, within the bound.
A program may use at most 128 MiB of HBM per device.

v0:
```python
import functools

import jax
import jax.numpy as jnp
from jax import lax
from jax.experimental import pallas as pl
from jax.experimental.pallas import tpu as pltpu
from jax.sharding import PartitionSpec as P

DH = 64
QLEN = 32
PAD = 2 * DH
MESH = pl.DeviceIdType.MESH
VM = pltpu.VMEM
DMA = pltpu.SemaphoreType.DMA

epsilon = 0.1


def normalize(matrix, gain_row):
    values = matrix.astype(jnp.float32)
    mean_square = jnp.mean(values * values, axis=-1, keepdims=True)
    return (values * lax.rsqrt(mean_square + epsilon) * gain_row).astype(jnp.bfloat16)


def place(n):
    me = lax.axis_index("mp")
    return me, me // 4, (me // 2) % 2, me % 2


def index_of(a, b, c):
    return (a * 2 + b) * 2 + c


def remote(src, dst, send, recv, to):
    return pltpu.make_async_remote_copy(
        src_ref=src, dst_ref=dst, send_sem=send, recv_sem=recv, device_id={"mp": to}, device_id_type=MESH
    )


def greet(to):
    pl.semaphore_signal(pltpu.get_barrier_semaphore(), inc=1, device_id={"mp": to}, device_id_type=MESH)


def gather_kernel(n, x_ref, out_ref, zs, zr, ys, yr, cs, cr):
    A = n // 4
    me, a, b, c = place(n)
    across, pair = index_of(a, 1 - b, c), index_of(a, b, 1 - c)
    right, left = me + 4, me - 4
    has = {1: a < A - 1, -1: a > 0}
    toward = {1: right, -1: left}
    for d in (1, -1):

        @pl.when(has[d])
        def _():
            greet(toward[d])

    greet(across)
    greet(pair)
    pl.semaphore_wait(
        pltpu.get_barrier_semaphore(), 2 + has[1].astype(jnp.int32) + has[-1].astype(jnp.int32)
    )

    def z_copy(src, k, s, d):
        row = 0 if d == 1 else A
        return remote(src, out_ref.at[index_of(k, b, c)], zs.at[row + s], zr.at[k], toward[d])

    def y_copy(src, k, bb):
        return remote(src, out_ref.at[index_of(k, bb, c)], ys.at[k], yr.at[k], across)

    def c_copy(src, k, bb, cc):
        return remote(src, out_ref.at[index_of(k, bb, cc)], cs.at[bb * A + k], cr.at[bb * A + k], pair)

    for d in (1, -1):

        @pl.when(has[d])
        def _():
            z_copy(x_ref, a, 0, d).start()

    y_copy(x_ref, a, b).start()
    c_copy(x_ref, a, b, c).start()
    out_ref[me] = x_ref[...]

    def pass_on(s):
        for d in (1, -1) if s else (1,):
            k = a - s * d

            @pl.when((k >= 0) & (k < A))
            def _():
                y_copy(x_ref, k, 1 - b).wait_recv()
                c_copy(out_ref.at[index_of(k, 1 - b, c)], k, 1 - b, c).start()

    for s in range(1, A):
        for d in (1, -1):
            k = a - s * d

            @pl.when((k >= 0) & (k < A))
            def _():
                block = out_ref.at[index_of(k, b, c)]
                remote(x_ref, block, zs.at[0], zr.at[k], toward[-d]).wait_recv()

                @pl.when(has[d])
                def _():
                    z_copy(block, k, s, d).start()

                y_copy(block, k, b).start()
                c_copy(block, k, b, c).start()

        pass_on(s - 1)
    pass_on(A - 1)
    for bb in range(2):
        for k in range(A):
            c_copy(x_ref, k, bb, 1 - c).wait_recv()
    for s in range(A):
        for d in (1, -1):
            k = a - s * d

            @pl.when((k >= 0) & (k < A) & has[d])
            def _():
                z_copy(x_ref, k, s, d).wait_send()

    for k in range(A):
        y_copy(x_ref, k, b).wait_send()
        for bb in range(2):
            c_copy(x_ref, k, bb, c).wait_send()


def params(number):
    return pltpu.CompilerParams(collective_id=number, has_side_effects=True, vmem_limit_bytes=56 * 2**20)


def gather(x, n, number):
    A = n // 4
    return pl.pallas_call(
        functools.partial(gather_kernel, n),
        out_shape=jax.ShapeDtypeStruct((n,) + x.shape, x.dtype),
        in_specs=[pl.BlockSpec(memory_space=VM)],
        out_specs=pl.BlockSpec(memory_space=VM),
        scratch_shapes=[DMA((2 * A,)), DMA((A,)), DMA((A,)), DMA((A,)), DMA((2 * A,)), DMA((2 * A,))],
        compiler_params=params(number),
        name=f"gather_{number}",
    )(x)


def scatter_kernel(
    n, left_ref, w_ref, out_ref, part, cbuf, ysend, yrecv, zsend, zright, zleft, cs, cr, ys, yr, zs, zr
):
    A = n // 4
    me, a, b, c = place(n)
    across, pair = index_of(a, 1 - b, c), index_of(a, b, 1 - c)
    has = {1: a < A - 1, -1: a > 0}
    toward = {1: me + 4, -1: me - 4}
    landing = {1: zright, -1: zleft}
    rows, width = out_ref.shape
    for d in (1, -1):

        @pl.when(has[d])
        def _():
            greet(toward[d])

    greet(across)
    greet(pair)
    pl.semaphore_wait(
        pltpu.get_barrier_semaphore(), 2 + has[1].astype(jnp.int32) + has[-1].astype(jnp.int32)
    )

    def near_last(visit):
        for s in range(A - 1, -1, -1):
            for d in (1, -1) if s else (1,):
                k = a + s * d

                @pl.when((k >= 0) & (k < A))
                def _():
                    visit(s, d, k)

    def multiply(group, bb, cc):
        left = jnp.concatenate([left_ref[index_of(k, bb, cc)] for k in range(A)], axis=0)
        tile = min(width, 1024)

        def columns(t, carry):
            at = pl.ds(pl.multiple_of(t * tile, tile), tile)
            found = jnp.dot(left, w_ref[:, at], preferred_element_type=jnp.float32)
            part[group, :, :, at] = found.reshape(A, rows, tile)
            return carry

        lax.fori_loop(0, width // tile, columns, 0)

    def c_copy(group, k, bb):
        slot = bb * A + k
        return remote(part.at[group, k], cbuf.at[slot], cs.at[slot], cr.at[slot], pair)

    def y_copy(k):
        return remote(ysend.at[k], yrecv.at[k], ys.at[k], yr.at[k], across)

    def z_copy(k, d):
        row = 0 if d == 1 else A
        return remote(zsend.at[k], landing[d].at[k], zs.at[k], zr.at[row + k], toward[d])

    def z_arrival(k, d):
        row = 0 if d == 1 else A
        return remote(zsend.at[k], landing[d].at[k], zs.at[k], zr.at[row + k], toward[-d])

    multiply(0, 1 - b, 1 - c)
    near_last(lambda s, d, k: c_copy(0, k, 1 - b).start())
    multiply(1, 1 - b, c)

    def send_across(s, d, k):
        c_copy(0, k, 1 - b).wait_recv()
        ysend[k] = (part[1, k] + cbuf[(1 - b) * A + k]).astype(jnp.bfloat16)
        y_copy(k).start()

    near_last(send_across)
    multiply(2, b, 1 - c)
    near_last(lambda s, d, k: c_copy(2, k, b).start())
    multiply(3, b, c)

    def pass_on(s, d, k):
        c_copy(2, k, b).wait_recv()
        y_copy(k).wait_recv()
        part[3, k] = part[3, k] + cbuf[b * A + k] + yrecv[k].astype(jnp.float32)
        for came in (d,) if s else (1, -1):

            @pl.when(has[-came])
            def _():
                z_arrival(k, came).wait_recv()
                part[3, k] = part[3, k] + landing[came][k].astype(jnp.float32)

        if s:
            zsend[k] = part[3, k].astype(jnp.bfloat16)
            z_copy(k, d).start()
        else:
            out_ref[...] = part[3, k]

    near_last(pass_on)

    def finish(s, d, k):
        y_copy(k).wait_send()
        if s:
            z_copy(k, d).wait_send()
        c_copy(0, k, 1 - b).wait_send()
        c_copy(2, k, b).wait_send()

    near_last(finish)


def scatter(left, w, n, number):
    A = n // 4
    rows, depth = left.shape[0] // n, left.shape[1]
    block = (rows, w.shape[1])
    half = jnp.bfloat16
    return pl.pallas_call(
        functools.partial(scatter_kernel, n),
        out_shape=jax.ShapeDtypeStruct(block, jnp.float32),
        in_specs=[pl.BlockSpec(memory_space=VM)] * 2,
        out_specs=pl.BlockSpec(memory_space=VM),
        scratch_shapes=[VM((4, A) + block, jnp.float32), VM((2 * A,) + block, jnp.float32)]
        + [VM((A,) + block, half)] * 5
        + [DMA((2 * A,)), DMA((2 * A,)), DMA((A,)), DMA((A,)), DMA((A,)), DMA((2 * A,))],
        compiler_params=params(number),
        name=f"scatter_{number}",
    )(left.reshape(n, rows, depth), w)


def attend_kernel(
    n, q_ref, own_ref, kv_ref, cached_ref, mask_ref, cached_mask_ref, out_ref,
    q_all, kv, cached, scores, chances, o_send, o_recv, st_send, st_recv, local, qs, qr, os, orr, ss, sr,
):
    me = lax.axis_index("mp")
    requests, positions, width = kv.shape
    pairs, heads = requests // 2, width // PAD
    load_cached = pltpu.make_async_copy(cached_ref, cached, local.at[0])
    load_kv = pltpu.make_async_copy(kv_ref, kv, local.at[1])
    load_cached.start()
    load_kv.start()
    order = sorted(range(1, n), key=lambda s: -min(s, n - s))
    others = [lax.rem(me + s, n) for s in order]
    for other in others:
        greet(other)
    pl.semaphore_wait(pltpu.get_barrier_semaphore(), n - 1)

    def q_copy(other, spot):
        return remote(q_ref, q_all.at[spot], qs.at[other], qr.at[spot], other)

    def o_copy(other, spot, step):
        rows = pl.ds(pl.multiple_of(step * QLEN, QLEN), QLEN)
        return remote(
            o_send.at[other, rows], o_recv.at[spot, rows], os.at[step, other], orr.at[step, spot], other
        )

    def st_copy(other, spot):
        return remote(st_send.at[other], st_recv.at[spot], ss.at[other], sr.at[spot], other)

    for other in others:
        q_copy(other, me).start()
    q_all[me] = q_ref[...]
    lane = lax.broadcasted_iota(jnp.int32, (QLEN, PAD), 1)
    load_cached.wait()

    def cached_request(r, carry):
        rows = pl.ds(pl.multiple_of(r * QLEN, QLEN), QLEN)
        block = cached[r]
        found = lax.dot_general(
            own_ref[rows, :], block, (((1,), (1,)), ((), ())), preferred_element_type=jnp.float32
        )
        usable = cached_mask_ref[r] > 0.5
        masked = jnp.where(usable, found, -1e30)
        exponent = jnp.where(usable, jnp.exp(masked - jnp.max(masked, axis=-1, keepdims=True)), 0.0)
        weights = (exponent / jnp.sum(exponent, axis=-1, keepdims=True)).astype(jnp.bfloat16)
        to = pl.ds(pl.multiple_of((requests + r) * QLEN, QLEN), QLEN)
        out_ref[to, :] = jnp.dot(weights, block, preferred_element_type=jnp.float32).astype(jnp.bfloat16)
        return carry

    lax.fori_loop(0, requests, cached_request, 0)
    st_send[...] = jnp.zeros_like(st_send)
    load_kv.wait()
    for other in others:
        q_copy(other, other).wait_recv()

    def pair_step(step, carry):
        rows = pl.ds(pl.multiple_of(step * QLEN, QLEN), QLEN)
        low = lane < DH
        nothing = jnp.zeros((QLEN, PAD), jnp.bfloat16)
        for i in range(2):
            for g in range(heads // 2):
                two = []
                for h in (2 * g, 2 * g + 1):
                    packed = q_all[h, rows, :].astype(jnp.float32)
                    packed = packed if i == 0 else pltpu.roll(packed, DH, 1)
                    two.append(jnp.where(low, packed, 0.0).astype(jnp.bfloat16))
                spread = jnp.concatenate(
                    [
                        jnp.concatenate([two[0], nothing], axis=1),
                        jnp.concatenate([nothing, two[1]], axis=1),
                    ],
                    axis=0,
                )
                scores[i, g] = lax.dot_general(
                    spread, kv[step * 2 + i, :, g * 2 * PAD : (g + 1) * 2 * PAD], (((1,), (1,)), ((), ())),
                    preferred_element_type=jnp.float32,
                )
        for i in range(2):
            r = step * 2 + i
            usable = mask_ref[r] > 0.5
            masked = jnp.where(usable, scores[i], -1e30)
            largest = jnp.max(masked, axis=-1, keepdims=True)
            exponent = jnp.where(usable, jnp.exp(masked - largest), 0.0)
            total = jnp.sum(exponent, axis=-1, keepdims=True)
            chances[i] = exponent.astype(jnp.bfloat16)
            st_send[...] = jnp.where(
                lane == r,
                largest.reshape(heads, QLEN, 1),
                jnp.where(lane == r + DH, total.reshape(heads, QLEN, 1), st_send[...]),
            )
        for g in range(heads // 2):
            found = [
                jnp.dot(
                    chances[i, g], kv[step * 2 + i, :, g * 2 * PAD : (g + 1) * 2 * PAD],
                    preferred_element_type=jnp.float32,
                )
                for i in range(2)
            ]
            for e in range(2):
                even, odd = (f[e * QLEN : (e + 1) * QLEN, e * PAD : (e + 1) * PAD] for f in found)
                o_send[2 * g + e, rows, :] = jnp.where(low, pltpu.roll(odd, DH, 1), even).astype(jnp.bfloat16)
        for other in others:
            o_copy(other, me, step).start()
        return carry

    lax.fori_loop(0, pairs, pair_step, 0)
    for other in others:
        st_copy(other, me).start()
    o_recv[me] = o_send[me]
    st_recv[me] = st_send[me]
    for other in others:
        st_copy(other, other).wait_recv()
    largest = st_recv[...]
    scale = jnp.exp(largest - jnp.max(largest, axis=0, keepdims=True))
    total = jnp.sum(
        scale * pltpu.roll(largest.reshape(n * QLEN, PAD), DH, 1).reshape(n, QLEN, PAD), axis=0, keepdims=True
    )
    st_recv[...] = scale / jnp.where(total > 0.0, total, 1.0)
    for step in range(pairs):
        for other in others:
            o_copy(other, other, step).wait_recv()
        mixed = jnp.zeros((QLEN, PAD), jnp.float32)
        for d in range(n):
            share = st_recv[d]
            share = jnp.where(
                lane < DH, share[:, 2 * step + 1 : 2 * step + 2], share[:, 2 * step : 2 * step + 1]
            )
            mixed = mixed + share * o_recv[d, step * QLEN : (step + 1) * QLEN, :].astype(jnp.float32)
        out_ref[2 * step * QLEN : (2 * step + 1) * QLEN, :] = mixed.astype(jnp.bfloat16)
        out_ref[(2 * step + 1) * QLEN : (2 * step + 2) * QLEN, :] = pltpu.roll(mixed, DH, 1).astype(jnp.bfloat16)
    for other in others:
        q_copy(other, me).wait_send()
        st_copy(other, me).wait_send()
        for step in range(pairs):
            o_copy(other, me, step).wait_send()


def attend(query, entering_kv, cached_kv, lengths, n, number):
    requests, positions, width = entering_kv.shape
    length = cached_kv.shape[1]
    pairs, heads = requests // 2, width // PAD
    half = query.shape[0] // 2
    packed = query[:half].reshape(pairs, 2, QLEN, DH)
    packed = jnp.concatenate([packed[:, 0], packed[:, 1]], axis=-1).reshape(pairs * QLEN, PAD)
    own = jnp.pad(query[half:], ((0, 0), (0, DH)))
    start = lax.axis_index("mp") * positions
    usable = (start + jnp.arange(positions, dtype=jnp.int32))[None, :] < lengths[0][:, None]
    cached_usable = jnp.arange(length, dtype=jnp.int32)[None, :] < lengths[1][:, None]
    half_type = jnp.bfloat16
    context = pl.pallas_call(
        functools.partial(attend_kernel, n),
        out_shape=jax.ShapeDtypeStruct((2 * requests * QLEN, PAD), half_type),
        in_specs=[pl.BlockSpec(memory_space=m) for m in (VM, VM, pl.ANY, pl.ANY, VM, VM)],
        out_specs=pl.BlockSpec(memory_space=VM),
        scratch_shapes=[
            VM((n,) + packed.shape, half_type),
            VM(entering_kv.shape, half_type),
            VM(cached_kv.shape, half_type),
            VM((2, heads // 2, 2 * QLEN, positions), jnp.float32),
            VM((2, heads // 2, 2 * QLEN, positions), half_type),
            VM((n, pairs * QLEN, PAD), half_type),
            VM((n, pairs * QLEN, PAD), half_type),
            VM((n, QLEN, PAD), jnp.float32),
            VM((n, QLEN, PAD), jnp.float32),
            DMA((2,)), DMA((n,)), DMA((n,)), DMA((pairs, n)), DMA((pairs, n)), DMA((n,)), DMA((n,)),
        ],
        compiler_params=params(number),
        name=f"attend_{number}",
    )(
        packed, own, entering_kv, cached_kv,
        usable.astype(jnp.float32)[:, None, :], cached_usable.astype(jnp.float32)[:, None, :],
    )
    return context[:, DH:]


def per_device(
    n,
    hidden,
    norm_gain_attn,
    w_query,
    entering_kv,
    cached_kv,
    enc_lengths,
    w_out,
    norm_gain_ffn,
    w_gate,
    w_up,
    w_down,
):
    width = hidden.shape[1]
    portion = gather(normalize(hidden, norm_gain_attn), n, 0).reshape(-1, width)
    query = jnp.dot(portion, w_query, preferred_element_type=jnp.float32).astype(jnp.bfloat16)
    context = attend(query, entering_kv, cached_kv, enc_lengths, n, 1)
    attention = scatter(context, w_out, n, 3)
    residual = (hidden.astype(jnp.float32) + attention).astype(jnp.bfloat16)
    portion = gather(normalize(residual, norm_gain_ffn), n, 4).reshape(-1, width)
    gate = jnp.dot(portion, w_gate, preferred_element_type=jnp.float32)
    upward = jnp.dot(portion, w_up, preferred_element_type=jnp.float32)
    activated = (jax.nn.gelu(gate, approximate=True) * upward).astype(jnp.bfloat16)
    feed_out = scatter(activated, w_down, n, 5)
    return (residual.astype(jnp.float32) + feed_out).astype(jnp.bfloat16)


def solution(mesh):
    placed = (
        P(("groups", "mp"), None),
        P(),
        P(None, "mp"),
        P("groups", "mp", None),
        P("groups", None, "mp"),
        P(None, "groups"),
        P("mp", None),
        P(),
        P(None, "mp"),
        P(None, "mp"),
        P("mp", None),
    )
    return jax.shard_map(
        functools.partial(per_device, mesh.shape["mp"]),
        mesh=mesh,
        in_specs=placed,
        out_specs=P(("groups", "mp"), None),
        check_vma=False,
    )
```

profile of v0, /device:TPU:0, one launch (start us, length us, event | category | flops | bytes accessed | tf_op | source)
XLA Modules:
  0.0 204.9 jit_solution(7742363975634259463)
XLA Ops:
  0.0 0.0 copy-start
  0.0 1.2 fusion.8
  1.2 0.8 slice_bitcast_fusion
  2.0 0.7 compare_convert_fusion.1.mask_ref
  2.6 0.7 compare_convert_fusion.cached_mask_ref
  3.3 1.8 fusion.10.x_ref
  5.1 35.0 %gather_0.1 = bf16[16,32,4096]{2,1,0:T(8,128)(2,1)} custom-call(bf16[32,4096]{1,0:T(8,128)(2,1)} %fusion.10.x_ref), custom_call_target="tpu_custom_call" | custom-call | tf_op jit(solution)/shard_map/gather_0/pallas_call | solution.py:134
  40.2 0.0 copy-done
  40.2 3.4 %convolution_convert_fusion = bf16[512,64]{1,0:T(8,128)(2,1)S(1)} fusion(bf16[512,4096]{1,0:T(8,128)(2,1)} %bitcast.20, bf16[4096,64]{0,1:T(8,128)(2,1)S(1)} %copy-done), kind=kOutput, calls=%fused_computation.10 | convolution fusion | flops 268468224 | bytes 4784128 | tf_op jit(solution)/shard_map/dot_general | solution.py:455
  43.6 0.6 pad.4.own_ref
  44.3 0.0 slice-start
  44.3 0.7 pad_maximum_fusion.q_ref
  45.0 0.0 copy-start.2
  45.0 0.0 copy-start.3
  45.0 0.0 slice-start.1
  45.0 38.3 %attend_1.1 = bf16[512,128]{1,0:T(8,128)(2,1)} custom-call(bf16[128,128]{1,0:T(8,128)(2,1)} %pad_maximum_fusion.q_ref, bf16[256,128]{1,0:T(8,128)(2,1)} %pad.4.own_ref, bf16[8,128,2048]{2,1,0:T(8,128)(2,1)} %kv_ref.1, bf16[8,2048,128]{2,1,0:T(8,128)(2,1)} %cached_ref.1, f32[8,1,128]{2,1,0:T(1,128)} %compare_convert_fusion.1.mask_ref, ...), custom_call_target="tpu_custom_call" | custom-call | tf_op jit(solution)/shard_map/attend_1/pallas_call | solution.py:413
  83.3 1.7 slice.27
  84.9 36.3 %scatter_3.1 = f32[32,4096]{1,0:T(8,128)} custom-call(bf16[16,32,64]{2,1,0:T(8,128)(2,1)} %bitcast.22, bf16[64,4096]{1,0:T(8,128)(2,1)} %w_ref.2), custom_call_target="tpu_custom_call" | custom-call | tf_op jit(solution)/shard_map/scatter_3/pallas_call | solution.py:251
  121.3 0.0 copy-done.2
  121.3 1.2 fusion.12
  122.5 0.0 copy-done.3
  122.5 0.8 fusion.14.x_ref
  123.4 31.9 %gather_4.1 = bf16[16,32,4096]{2,1,0:T(8,128)(2,1)} custom-call(bf16[32,4096]{1,0:T(8,128)(2,1)} %fusion.14.x_ref), custom_call_target="tpu_custom_call" | custom-call | tf_op jit(solution)/shard_map/gather_4/pallas_call | solution.py:134
  155.2 0.0 slice-done
  155.2 0.0 slice-done.1
  155.3 0.0 copy-start.1
  155.3 5.5 %fusion.19 = f32[512,640]{1,0:T(8,128)S(1)} fusion(bf16[512,4096]{1,0:T(8,128)(2,1)} %bitcast.18, bf16[4096,640]{1,0:T(8,128)(2,1)S(1)} %bitcast.28), kind=kOutput, calls=%fused_computation.35 | convolution fusion | flops 2684354560 | bytes 10747904 | tf_op jit(solution)/shard_map/dot_general | solution.py:460
  160.7 0.0 copy-done.1
  160.8 6.9 %fusion = bf16[512,640]{1,0:T(8,128)(2,1)} fusion(bf16[512,4096]{1,0:T(8,128)(2,1)S(1)} %bitcast.19, bf16[4096,640]{1,0:T(8,128)(2,1)} %param.20, f32[512,640]{1,0:T(8,128)S(1)} %fusion.19), kind=kOutput, calls=%fused_computation.2 | convolution fusion | flops 2687631360 | bytes 11403264 | tf_op jit(solution)/shard_map/dot_general | solution.py:461
  167.6 35.4 %scatter_5.1 = f32[32,4096]{1,0:T(8,128)} custom-call(bf16[16,32,640]{2,1,0:T(8,128)(2,1)} %bitcast.21, bf16[640,4096]{1,0:T(8,128)(2,1)} %w_ref.3), custom_call_target="tpu_custom_call" | custom-call | tf_op jit(solution)/shard_map/scatter_5/pallas_call | solution.py:251
  203.1 1.8 fusion.15
  (7 shorter events, 0.0 us)
Async XLA Ops:
  0.0 40.2 %copy-start = (bf16[4096,64]{0,1:T(8,128)(2,1)S(1)}, bf16[4096,64]{0,1:T(8,128)(2,1)}, u32[]{:S(2)}) copy-start(bf16[4096,64]{0,1:T(8,128)(2,1)} %param.13) | copy-start | bytes 1572868
  44.3 111.0 %slice-start = ((s8[5242880]{0:T(1024)(128)(4,1)}), s8[4194304]{0:T(1024)(128)(4,1)S(1)}, s32[]{:S(2)}) async-start(s8[5242880]{0:T(1024)(128)(4,1)} %bitcast.27), calls=%async_computation | async-start | bytes 8388608
  45.0 76.3 %copy-start.2 = (bf16[32,4096]{1,0:T(8,128)(2,1)S(1)}, bf16[32,4096]{1,0:T(8,128)(2,1)}, u32[]{:S(2)}) copy-start(bf16[32,4096]{1,0:T(8,128)(2,1)} %param.11) | copy-start | bytes 786436
  45.0 77.6 %copy-start.3 = (f32[4096]{0:T(1024)S(1)}, f32[4096]{0:T(1024)}, u32[]{:S(2)}) copy-start(f32[4096]{0:T(1024)} %param.18) | copy-start | bytes 49156
  45.0 110.3 %slice-start.1 = ((s8[5242880]{0:T(1024)(128)(4,1)}), s8[1048576]{0:T(1024)(128)(4,1)S(1)}, s32[]{:S(2)}) async-start(s8[5242880]{0:T(1024)(128)(4,1)} %bitcast.27), calls=%async_computation.1 | async-start | bytes 2097152
  155.3 5.5 %copy-start.1 = (bf16[16,32,4096]{2,1,0:T(8,128)(2,1)S(1)}, bf16[16,32,4096]{2,1,0:T(8,128)(2,1)}, u32[]{:S(2)}) copy-start(bf16[16,32,4096]{2,1,0:T(8,128)(2,1)} %gather_4.1) | copy-start | bytes 12582916
where the time goes:
time: 205 us
  Pallas kernels  177 us (86%)
  matrix products  15.8 us (8%)
  other arithmetic  8.91 us (4%)
  local copies, waits for them, and re-layouts  3.12 us (2%)
    pallas_call x2, Pallas kernels, scatter(): pl.pallas_call(functools.partial(scatter_kernel, n), out_shape=jax.ShapeD...  71.7 us
    pallas_call x2, Pallas kernels, gather(): pl.pallas_call(functools.partial(gather_kernel, n), out_shape=jax.ShapeDt...  66.9 us
    pallas_call x1, Pallas kernels, attend(): pl.pallas_call(functools.partial(attend_kernel, n), out_shape=jax.ShapeDt...  38.3 us
    dot_general x1, matrix products, per_device(): upward = jnp.dot(portion, w_up, preferred_element_type=jnp.float32)  6.89 us
    dot_general x1, matrix products, per_device(): gate = jnp.dot(portion, w_gate, preferred_element_type=jnp.float32)  5.46 us

commit v1 on v0

--- a/solution.py
+++ b/solution.py
@@ -261,9 +261,276 @@
     )(left.reshape(n, rows, depth), w)
 
 
+def pieces_of(n, width):
+    return max(1, min(4, 16 // (n // 4), width // 128))
+
+
+def neighbours(n):
+    A = n // 4
+    me, a, b, c = place(n)
+    has = {1: a < A - 1, -1: a > 0}
+    toward = {1: me + 4, -1: me - 4}
+    return has, toward
+
+
+def greet_along(has, toward):
+    for d in (1, -1):
+
+        @pl.when(has[d])
+        def _():
+            greet(toward[d])
+
+
+def await_greetings(has, others):
+    pl.semaphore_wait(
+        pltpu.get_barrier_semaphore(), others + has[1].astype(jnp.int32) + has[-1].astype(jnp.int32)
+    )
+
+
+def query_kernel(
+    n, x_ref, gain_ref, wq_ref, wo_ref, q_ref, plane_ref,
+    xs, w2, q_send, q_recv, local, zs, zr, cs, cr, ws, wr, ps, pr,
+):
+    A = n // 4
+    me, a, b, c = place(n)
+    across, pair = index_of(a, 1 - b, c), index_of(a, b, 1 - c)
+    has, toward = neighbours(n)
+    P, W = xs.shape[0], xs.shape[-1]
+    rows = x_ref.shape[0]
+    greet_along(has, toward)
+    greet(across)
+    greet(pair)
+    load_w = pltpu.make_async_copy(wq_ref, w2.at[0], local.at[0])
+    load_w.start()
+    values = x_ref[...].astype(jnp.float32)
+    scale = lax.rsqrt(jnp.mean(values * values, axis=-1, keepdims=True) + epsilon)
+    for p in range(P):
+        part = slice(p * W, (p + 1) * W)
+        xs[p, a, c] = (values[:, part] * scale * gain_ref[:, part]).astype(jnp.bfloat16)
+    await_greetings(has, 2)
+
+    def z_copy(k, p, s, d):
+        row = 0 if d == 1 else A
+        return remote(xs.at[p, k, c], xs.at[p, k, c], zs.at[row + s, p], zr.at[k, p], toward[d])
+
+    def c_copy(k, p, cc):
+        return remote(xs.at[p, k, cc], xs.at[p, k, cc], cs.at[k, p], cr.at[k, p], pair)
+
+    wq_copy = remote(wq_ref, w2.at[1], ws.at[0], wr.at[0], across)
+    q_copy = remote(q_send, q_recv, ws.at[1], wr.at[1], across)
+    plane_pair = remote(wo_ref, plane_ref.at[0], ps.at[0], pr.at[0], pair)
+    plane_across = remote(wo_ref, plane_ref.at[1], ps.at[1], pr.at[1], across)
+    plane_diagonal = remote(plane_ref.at[1], plane_ref.at[2], ps.at[2], pr.at[2], pair)
+    for p in range(P):
+        for d in (1, -1):
+
+            @pl.when(has[d])
+            def _():
+                z_copy(a, p, 0, d).start()
+
+    wq_copy.start()
+    plane_across.start()
+    for p in range(P):
+        c_copy(a, p, c).start()
+    plane_pair.start()
+    for s in range(1, A):
+        for p in range(P):
+            for d in (1, -1):
+                k = a - s * d
+
+                @pl.when((k >= 0) & (k < A))
+                def _():
+                    remote(xs.at[p, k, c], xs.at[p, k, c], zs.at[0, p], zr.at[k, p], toward[-d]).wait_recv()
+
+                    @pl.when(has[d])
+                    def _():
+                        z_copy(k, p, s, d).start()
+
+                    c_copy(k, p, c).start()
+
+    load_w.wait()
+    wq_copy.wait_recv()
+    for k in range(A):
+        for p in range(P):
+            c_copy(k, p, 1 - c).wait_recv()
+    total = jnp.zeros((2 * A * rows, PAD), jnp.float32)
+    for p in range(P):
+        total = total + lax.dot_general(
+            xs[p].reshape(2 * A * rows, W), w2[:, :, p * W : (p + 1) * W].reshape(PAD, W),
+            (((1,), (1,)), ((), ())), preferred_element_type=jnp.float32,
+        )
+    q_send[...] = total.astype(jnp.bfloat16)
+    low = lax.broadcasted_iota(jnp.int32, (2 * A * rows, PAD), 1) < DH
+    own = jnp.where(low, total, 0.0).astype(jnp.bfloat16).reshape(2 * A, rows, PAD)
+    for k in range(A):
+        for cc in range(2):
+            q_ref[index_of(k, b, cc)] = own[2 * k + cc]
+    q_copy.start()
+    plane_across.wait_recv()
+    plane_diagonal.start()
+    for s in range(A):
+        for d in (1, -1):
+            k = a - s * d
+
+            @pl.when((k >= 0) & (k < A) & has[d])
+            def _():
+                for p in range(P):
+                    z_copy(k, p, s, d).wait_send()
+
+    for k in range(A):
+        for p in range(P):
+            c_copy(k, p, c).wait_send()
+    q_copy.wait_recv()
+    came = pltpu.roll(q_recv[...].astype(jnp.float32), DH, 1)
+    came = jnp.where(low, came, 0.0).astype(jnp.bfloat16).reshape(2 * A, rows, PAD)
+    for k in range(A):
+        for cc in range(2):
+            q_ref[index_of(k, 1 - b, cc)] = came[2 * k + cc]
+    wq_copy.wait_send()
+    q_copy.wait_send()
+    plane_across.wait_send()
+    plane_pair.wait()
+    plane_diagonal.wait()
+
+
+def make_query(hidden, gain, w_query, w_out, n, number):
+    A = n // 4
+    rows, width = hidden.shape
+    P = pieces_of(n, width)
+    W = width // P
+    half = jnp.bfloat16
+    return pl.pallas_call(
+        functools.partial(query_kernel, n),
+        out_shape=[
+            jax.ShapeDtypeStruct((n, rows, PAD), half),
+            jax.ShapeDtypeStruct((3,) + w_out.shape, half),
+        ],
+        in_specs=[pl.BlockSpec(memory_space=m) for m in (VM, VM, pl.ANY, pl.ANY)],
+        out_specs=[pl.BlockSpec(memory_space=VM), pl.BlockSpec(memory_space=pl.ANY)],
+        scratch_shapes=[
+            VM((P, A, 2, rows, W), half),
+            VM((2, DH, width), half),
+            VM((2 * A * rows, PAD), half),
+            VM((2 * A * rows, PAD), half),
+            DMA((1,)), DMA((2 * A, P)), DMA((A, P)), DMA((A, P)), DMA((A, P)),
+            DMA((2,)), DMA((2,)), DMA((3,)), DMA((3,)),
+        ],
+        compiler_params=params(number),
+        name=f"query_{number}",
+    )(hidden, gain[None, :], w_query.T, w_out)
+
+
+def project_kernel(
+    n, context_ref, hidden_ref, wo_ref, plane_ref, out_ref,
+    w4, c_send, c_recv, part, zsend, zright, zleft, local, cs, cr, zs, zr,
+):
+    A = n // 4
+    me, a, b, c = place(n)
+    peers = (index_of(a, b, 1 - c), index_of(a, 1 - b, c), index_of(a, 1 - b, 1 - c))
+    has, toward = neighbours(n)
+    landing = {1: zright, -1: zleft}
+    P, _, rows, W = part.shape
+    depth = wo_ref.shape[0]
+    greet_along(has, toward)
+    for peer in peers:
+        greet(peer)
+    load_own = pltpu.make_async_copy(wo_ref, w4.at[0], local.at[0])
+    load_plane = pltpu.make_async_copy(plane_ref, w4.at[pl.ds(1, 3)], local.at[1])
+    load_own.start()
+    load_plane.start()
+    for i, (bb, cc) in enumerate(((b, 1 - c), (1 - b, c), (1 - b, 1 - c))):
+        for k in range(A):
+            c_send[i, k] = context_ref[index_of(k, bb, cc)]
+    for k in range(A):
+        c_recv[0, k] = context_ref[index_of(k, b, c)]
+    await_greetings(has, 3)
+    swaps = [remote(c_send.at[i], c_recv.at[i + 1], cs.at[i], cr.at[i], peers[i]) for i in range(3)]
+    for i in (2, 1, 0):
+        swaps[i].start()
+    load_own.wait()
+    load_plane.wait()
+    for swap in swaps:
+        swap.wait_recv()
+    low = lax.broadcasted_iota(jnp.int32, (A * rows, PAD), 1) < DH
+
+    def beside(i):
+        first = c_recv[i].reshape(A * rows, PAD).astype(jnp.float32)
+        second = c_recv[i + 1].reshape(A * rows, PAD).astype(jnp.float32)
+        return jnp.where(low, pltpu.roll(first, DH, 1), second).astype(jnp.bfloat16)
+
+    left = jnp.concatenate([beside(0), beside(2)], axis=1)
+
+    def z_copy(k, p, d):
+        return remote(zsend.at[p, k], landing[d].at[p, k], zs.at[k, p], zr.at[(0 if d == 1 else A) + k, p], toward[d])
+
+    def z_arrival(k, p, d):
+        return remote(zsend.at[p, k], landing[d].at[p, k], zs.at[k, p], zr.at[(0 if d == 1 else A) + k, p], toward[-d])
+
+    for s in range(A - 1, -1, -1):
+        for p in range(P):
+            if s == A - 1:
+                w = w4[:, :, p * W : (p + 1) * W].reshape(4 * depth, W)
+                found = jnp.dot(left, w, preferred_element_type=jnp.float32)
+                part[p] = found.reshape(A, rows, W)
+            for d in (1, -1) if s else (1,):
+                k = a + s * d
+
+                @pl.when((k >= 0) & (k < A))
+                def _():
+                    for came in (d,) if s else (1, -1):
+
+                        @pl.when(has[-came])
+                        def _():
+                            z_arrival(k, p, came).wait_recv()
+                            part[p, k] = part[p, k] + landing[came][p, k].astype(jnp.float32)
+
+                    if s:
+                        zsend[p, k] = part[p, k].astype(jnp.bfloat16)
+                        z_copy(k, p, d).start()
+                    else:
+                        at = slice(p * W, (p + 1) * W)
+                        out_ref[:, at] = (hidden_ref[:, at].astype(jnp.float32) + part[p, k]).astype(jnp.bfloat16)
+
+    for s in range(A - 1, 0, -1):
+        for d in (1, -1):
+            k = a + s * d
+
+            @pl.when((k >= 0) & (k < A))
+            def _():
+                for p in range(P):
+                    z_copy(k, p, d).wait_send()
+
+    for swap in swaps:
+        swap.wait_send()
+
+
+def project(context, hidden, w_out, plane, n, number):
+    A = n // 4
+    rows, width = hidden.shape
+    P = pieces_of(n, width)
+    W = width // P
+    half = jnp.bfloat16
+    return pl.pallas_call(
+        functools.partial(project_kernel, n),
+        out_shape=jax.ShapeDtypeStruct((rows, width), half),
+        in_specs=[pl.BlockSpec(memory_space=m) for m in (VM, VM, pl.ANY, pl.ANY)],
+        out_specs=pl.BlockSpec(memory_space=VM),
+        scratch_shapes=[
+            VM((4,) + w_out.shape, half),
+            VM((3, A, rows, PAD), half),
+            VM((4, A, rows, PAD), half),
+            VM((P, A, rows, W), jnp.float32),
+        ]
+        + [VM((P, A, rows, W), half)] * 3
+        + [DMA((2,)), DMA((3,)), DMA((3,)), DMA((A, P)), DMA((2 * A, P))],
+        compiler_params=params(number),
+        name=f"project_{number}",
+    )(context, hidden, w_out, plane)
+
+
 def attend_kernel(
-    n, q_ref, own_ref, kv_ref, cached_ref, mask_ref, cached_mask_ref, out_ref,
-    q_all, kv, cached, scores, chances, o_send, o_recv, st_send, st_recv, local, qs, qr, os, orr, ss, sr,
+    n, own_ref, kv_ref, cached_ref, mask_ref, cached_mask_ref, out_ref,
+    q_ref, q_all, kv, cached, scores, chances, o_send, o_recv, st_send, st_recv, local, qs, qr, os, orr, ss, sr,
 ):
     me = lax.axis_index("mp")
     requests, positions, width = kv.shape
@@ -276,6 +543,11 @@
     others = [lax.rem(me + s, n) for s in order]
     for other in others:
         greet(other)
+    for step in range(pairs):
+        even, odd = (
+            own_ref[(2 * step + i) * QLEN : (2 * step + i + 1) * QLEN, :].astype(jnp.float32) for i in range(2)
+        )
+        q_ref[step * QLEN : (step + 1) * QLEN, :] = (even + pltpu.roll(odd, DH, 1)).astype(jnp.bfloat16)
     pl.semaphore_wait(pltpu.get_barrier_semaphore(), n - 1)
 
     def q_copy(other, spot):
@@ -297,16 +569,15 @@
     load_cached.wait()
 
     def cached_request(r, carry):
-        rows = pl.ds(pl.multiple_of(r * QLEN, QLEN), QLEN)
+        to = pl.ds(pl.multiple_of((requests + r) * QLEN, QLEN), QLEN)
         block = cached[r]
         found = lax.dot_general(
-            own_ref[rows, :], block, (((1,), (1,)), ((), ())), preferred_element_type=jnp.float32
+            own_ref[to, :], block, (((1,), (1,)), ((), ())), preferred_element_type=jnp.float32
         )
         usable = cached_mask_ref[r] > 0.5
         masked = jnp.where(usable, found, -1e30)
         exponent = jnp.where(usable, jnp.exp(masked - jnp.max(masked, axis=-1, keepdims=True)), 0.0)
         weights = (exponent / jnp.sum(exponent, axis=-1, keepdims=True)).astype(jnp.bfloat16)
-        to = pl.ds(pl.multiple_of((requests + r) * QLEN, QLEN), QLEN)
         out_ref[to, :] = jnp.dot(weights, block, preferred_element_type=jnp.float32).astype(jnp.bfloat16)
         return carry
 
@@ -402,10 +673,6 @@
     requests, positions, width = entering_kv.shape
     length = cached_kv.shape[1]
     pairs, heads = requests // 2, width // PAD
-    half = query.shape[0] // 2
-    packed = query[:half].reshape(pairs, 2, QLEN, DH)
-    packed = jnp.concatenate([packed[:, 0], packed[:, 1]], axis=-1).reshape(pairs * QLEN, PAD)
-    own = jnp.pad(query[half:], ((0, 0), (0, DH)))
     start = lax.axis_index("mp") * positions
     usable = (start + jnp.arange(positions, dtype=jnp.int32))[None, :] < lengths[0][:, None]
     cached_usable = jnp.arange(length, dtype=jnp.int32)[None, :] < lengths[1][:, None]
@@ -413,10 +680,11 @@
     context = pl.pallas_call(
         functools.partial(attend_kernel, n),
         out_shape=jax.ShapeDtypeStruct((2 * requests * QLEN, PAD), half_type),
-        in_specs=[pl.BlockSpec(memory_space=m) for m in (VM, VM, pl.ANY, pl.ANY, VM, VM)],
+        in_specs=[pl.BlockSpec(memory_space=m) for m in (VM, pl.ANY, pl.ANY, VM, VM)],
         out_specs=pl.BlockSpec(memory_space=VM),
         scratch_shapes=[
-            VM((n,) + packed.shape, half_type),
+            VM((pairs * QLEN, PAD), half_type),
+            VM((n, pairs * QLEN, PAD), half_type),
             VM(entering_kv.shape, half_type),
             VM(cached_kv.shape, half_type),
             VM((2, heads // 2, 2 * QLEN, positions), jnp.float32),
@@ -430,10 +698,10 @@
         compiler_params=params(number),
         name=f"attend_{number}",
     )(
-        packed, own, entering_kv, cached_kv,
+        query, entering_kv, cached_kv,
         usable.astype(jnp.float32)[:, None, :], cached_usable.astype(jnp.float32)[:, None, :],
     )
-    return context[:, DH:]
+    return context
 
 
 def per_device(
@@ -450,12 +718,10 @@
     w_up,
     w_down,
 ):
-    width = hidden.shape[1]
-    portion = gather(normalize(hidden, norm_gain_attn), n, 0).reshape(-1, width)
-    query = jnp.dot(portion, w_query, preferred_element_type=jnp.float32).astype(jnp.bfloat16)
-    context = attend(query, entering_kv, cached_kv, enc_lengths, n, 1)
-    attention = scatter(context, w_out, n, 3)
-    residual = (hidden.astype(jnp.float32) + attention).astype(jnp.bfloat16)
+    rows, width = hidden.shape
+    query, plane = make_query(hidden, norm_gain_attn, w_query, w_out, n, 0)
+    context = attend(query.reshape(-1, PAD), entering_kv, cached_kv, enc_lengths, n, 1)
+    residual = project(context.reshape(n, rows, PAD), hidden, w_out, plane, n, 3)
     portion = gather(normalize(residual, norm_gain_ffn), n, 4).reshape(-1, width)
     gate = jnp.dot(portion, w_gate, preferred_element_type=jnp.float32)
     upward = jnp.dot(portion, w_up, preferred_element_type=jnp.float32)

time: 205 us -> 185 us (0.902)
  Pallas kernels: 177 us -> 165 us
  matrix products: 15.8 us -> 12.4 us
  other arithmetic: 8.91 us -> 6.1 us
  local copies, waits for them, and re-layouts: 3.12 us -> 0.78 us
    pallas_call x0 -> x2, Pallas kernels: none -> 57.2 us  [the longest x1 32.9 us: make_query(): pl.pallas_call(functools.partial(query_kernel, n), out_shape=[jax.ShapeDt...]
    pallas_call x2 -> x1, Pallas kernels: 71.7 us -> 35.4 us  [scatter(): pl.pallas_call(functools.partial(scatter_kernel, n), out_shape=jax.ShapeD...]
    pallas_call x2 -> x1, Pallas kernels: 66.9 us -> 33 us  [gather(): pl.pallas_call(functools.partial(gather_kernel, n), out_shape=jax.ShapeDt...]
    dot_general x1 -> x0, matrix products: 3.42 us -> none  [per_device(): jnp.dot(portion, w_query, preferred_element_type=jnp.float32)]
where the time goes in v1:
time: 185 us; the launch traced here: 184 us
  Pallas kernels  165 us (89%)
  matrix products  12.4 us (7%)
  other arithmetic  6.1 us (3%)
    pallas_call x1, Pallas kernels, attend(): pl.pallas_call(functools.partial(attend_kernel, n), out_shape=jax.ShapeDt...  39.5 us
    pallas_call x1, Pallas kernels, scatter(): pl.pallas_call(functools.partial(scatter_kernel, n), out_shape=jax.ShapeD...  35.4 us
    pallas_call x1, Pallas kernels, gather(): pl.pallas_call(functools.partial(gather_kernel, n), out_shape=jax.ShapeDt...  33 us
    pallas_call x1, Pallas kernels, make_query(): pl.pallas_call(functools.partial(query_kernel, n), out_shape=[jax.ShapeDt...  32.9 us
    pallas_call x1, Pallas kernels, project(): pl.pallas_call(functools.partial(project_kernel, n), out_shape=jax.ShapeD...  24.3 us
    dot_general x1, matrix products, per_device(): upward = jnp.dot(portion, w_up, preferred_element_type=jnp.float32)  6.89 us
    dot_general x1, matrix products, per_device(): gate = jnp.dot(portion, w_gate, preferred_element_type=jnp.float32)  5.46 us

profile of v1, /device:TPU:0, one launch (start us, length us, event | category | flops | bytes accessed | tf_op | source)
XLA Modules:
  0.0 184.5 jit_solution(2823653433057398653)
XLA Ops:
  0.0 0.8 slice_bitcast_fusion
  0.8 0.7 compare_convert_fusion.1.mask_ref
  1.4 0.7 compare_convert_fusion.cached_mask_ref
  2.2 0.0 slice-start
  2.2 32.9 %query_0.1 = (bf16[16,32,128]{2,1,0:T(8,128)(2,1)}, bf16[3,64,4096]{2,1,0:T(8,128)(2,1)}) custom-call(bf16[32,4096]{1,0:T(8,128)(2,1)} %hidden_ref.1, f32[1,4096]{1,0:T(1,128)} %bitcast.22, bf16[64,4096]{1,0:T(8,128)(2,1)} %bitcast.19, bf16[64,4096]{1,0:T(8,128)(2,1)} %wo_ref.3), custom_call_target="tpu_custom_call" | custom-call | tf_op jit(solution)/shard_map/query_0/pallas_call | solution.py:402
  35.1 0.0 slice-start.1
  35.1 39.5 %attend_1.1 = bf16[512,128]{1,0:T(8,128)(2,1)} custom-call(bf16[512,128]{1,0:T(8,128)(2,1)} %bitcast.20, bf16[8,128,2048]{2,1,0:T(8,128)(2,1)} %kv_ref.1, bf16[8,2048,128]{2,1,0:T(8,128)(2,1)} %cached_ref.1, f32[8,1,128]{2,1,0:T(1,128)} %compare_convert_fusion.1.mask_ref, f32[8,1,2048]{2,1,0:T(1,128)} %compare_convert_fusion.cached_mask_ref), custom_call_target="tpu_custom_call" | custom-call | tf_op jit(solution)/shard_map/attend_1/pallas_call | solution.py:680
  74.6 0.0 copy-start.2
  74.6 24.3 %project_3.1 = bf16[32,4096]{1,0:T(8,128)(2,1)} custom-call(bf16[16,32,128]{2,1,0:T(8,128)(2,1)} %bitcast.18, bf16[32,4096]{1,0:T(8,128)(2,1)} %hidden_ref.1, bf16[64,4096]{1,0:T(8,128)(2,1)} %wo_ref.3, bf16[3,64,4096]{2,1,0:T(8,128)(2,1)} %get-tuple-element.8.plane_ref), custom_call_target="tpu_custom_call" | custom-call | tf_op jit(solution)/shard_map/project_3/pallas_call | solution.py:513
  98.9 1.1 fusion.8
  100.1 0.0 copy-done.2
  100.1 1.8 fusion.10.x_ref
  101.8 33.0 %gather_4.1 = bf16[16,32,4096]{2,1,0:T(8,128)(2,1)} custom-call(bf16[32,4096]{1,0:T(8,128)(2,1)} %fusion.10.x_ref), custom_call_target="tpu_custom_call" | custom-call | tf_op jit(solution)/shard_map/gather_4/pallas_call | solution.py:134
  134.8 0.0 slice-done
  134.8 0.0 slice-done.1
  134.9 0.0 copy-start
  134.9 5.5 %fusion.12 = f32[512,640]{1,0:T(8,128)S(1)} fusion(bf16[512,4096]{1,0:T(8,128)(2,1)} %bitcast.15, bf16[4096,640]{1,0:T(8,128)(2,1)S(1)} %bitcast.24), kind=kOutput, calls=%fused_computation.23 | convolution fusion | flops 2684354560 | bytes 10747904 | tf_op jit(solution)/shard_map/dot_general | solution.py:726
  140.3 0.0 copy-done
  140.4 6.9 %fusion = bf16[512,640]{1,0:T(8,128)(2,1)} fusion(bf16[512,4096]{1,0:T(8,128)(2,1)S(1)} %bitcast.16, bf16[4096,640]{1,0:T(8,128)(2,1)} %param.20, f32[512,640]{1,0:T(8,128)S(1)} %fusion.12), kind=kOutput, calls=%fused_computation.2 | convolution fusion | flops 2687631360 | bytes 11403264 | tf_op jit(solution)/shard_map/dot_general | solution.py:727
  147.2 0.0 copy-start.1
  147.2 35.4 %scatter_5.1 = f32[32,4096]{1,0:T(8,128)} custom-call(bf16[16,32,640]{2,1,0:T(8,128)(2,1)} %bitcast.17, bf16[640,4096]{1,0:T(8,128)(2,1)} %w_ref.1), custom_call_target="tpu_custom_call" | custom-call | tf_op jit(solution)/shard_map/scatter_5/pallas_call | solution.py:251
  182.7 0.0 copy-done.1
  182.7 1.8 fusion.11
  (4 shorter events, 0.0 us)
Async XLA Ops:
  2.2 132.7 %slice-start = ((s8[5242880]{0:T(1024)(128)(4,1)}), s8[4194304]{0:T(1024)(128)(4,1)S(1)}, s32[]{:S(2)}) async-start(s8[5242880]{0:T(1024)(128)(4,1)} %bitcast.23), calls=%async_computation | async-start | bytes 8388608
  35.1 99.8 %slice-start.1 = ((s8[5242880]{0:T(1024)(128)(4,1)}), s8[1048576]{0:T(1024)(128)(4,1)S(1)}, s32[]{:S(2)}) async-start(s8[5242880]{0:T(1024)(128)(4,1)} %bitcast.23), calls=%async_computation.1 | async-start | bytes 2097152
  74.6 25.4 %copy-start.2 = (f32[4096]{0:T(1024)S(1)}, f32[4096]{0:T(1024)}, u32[]{:S(2)}) copy-start(f32[4096]{0:T(1024)} %param.18) | copy-start | bytes 49156
  134.9 5.5 %copy-start = (bf16[16,32,4096]{2,1,0:T(8,128)(2,1)S(1)}, bf16[16,32,4096]{2,1,0:T(8,128)(2,1)}, u32[]{:S(2)}) copy-start(bf16[16,32,4096]{2,1,0:T(8,128)(2,1)} %gather_4.1) | copy-start | bytes 12582916
  147.2 35.5 %copy-start.1 = (bf16[32,4096]{1,0:T(8,128)(2,1)S(1)}, bf16[32,4096]{1,0:T(8,128)(2,1)}, u32[]{:S(2)}) copy-start(bf16[32,4096]{1,0:T(8,128)(2,1)} %project_3.1) | copy-start | bytes 786436

commit v2 on v1

--- a/solution.py
+++ b/solution.py
@@ -17,12 +17,6 @@
 epsilon = 0.1
 
 
-def normalize(matrix, gain_row):
-    values = matrix.astype(jnp.float32)
-    mean_square = jnp.mean(values * values, axis=-1, keepdims=True)
-    return (values * lax.rsqrt(mean_square + epsilon) * gain_row).astype(jnp.bfloat16)
-
-
 def place(n):
     me = lax.axis_index("mp")
     return me, me // 4, (me // 2) % 2, me % 2
@@ -42,223 +36,8 @@
     pl.semaphore_signal(pltpu.get_barrier_semaphore(), inc=1, device_id={"mp": to}, device_id_type=MESH)
 
 
-def gather_kernel(n, x_ref, out_ref, zs, zr, ys, yr, cs, cr):
-    A = n // 4
-    me, a, b, c = place(n)
-    across, pair = index_of(a, 1 - b, c), index_of(a, b, 1 - c)
-    right, left = me + 4, me - 4
-    has = {1: a < A - 1, -1: a > 0}
-    toward = {1: right, -1: left}
-    for d in (1, -1):
-
-        @pl.when(has[d])
-        def _():
-            greet(toward[d])
-
-    greet(across)
-    greet(pair)
-    pl.semaphore_wait(
-        pltpu.get_barrier_semaphore(), 2 + has[1].astype(jnp.int32) + has[-1].astype(jnp.int32)
-    )
-
-    def z_copy(src, k, s, d):
-        row = 0 if d == 1 else A
-        return remote(src, out_ref.at[index_of(k, b, c)], zs.at[row + s], zr.at[k], toward[d])
-
-    def y_copy(src, k, bb):
-        return remote(src, out_ref.at[index_of(k, bb, c)], ys.at[k], yr.at[k], across)
-
-    def c_copy(src, k, bb, cc):
-        return remote(src, out_ref.at[index_of(k, bb, cc)], cs.at[bb * A + k], cr.at[bb * A + k], pair)
-
-    for d in (1, -1):
-
-        @pl.when(has[d])
-        def _():
-            z_copy(x_ref, a, 0, d).start()
-
-    y_copy(x_ref, a, b).start()
-    c_copy(x_ref, a, b, c).start()
-    out_ref[me] = x_ref[...]
-
-    def pass_on(s):
-        for d in (1, -1) if s else (1,):
-            k = a - s * d
-
-            @pl.when((k >= 0) & (k < A))
-            def _():
-                y_copy(x_ref, k, 1 - b).wait_recv()
-                c_copy(out_ref.at[index_of(k, 1 - b, c)], k, 1 - b, c).start()
-
-    for s in range(1, A):
-        for d in (1, -1):
-            k = a - s * d
-
-            @pl.when((k >= 0) & (k < A))
-            def _():
-                block = out_ref.at[index_of(k, b, c)]
-                remote(x_ref, block, zs.at[0], zr.at[k], toward[-d]).wait_recv()
-
-                @pl.when(has[d])
-                def _():
-                    z_copy(block, k, s, d).start()
-
-                y_copy(block, k, b).start()
-                c_copy(block, k, b, c).start()
-
-        pass_on(s - 1)
-    pass_on(A - 1)
-    for bb in range(2):
-        for k in range(A):
-            c_copy(x_ref, k, bb, 1 - c).wait_recv()
-    for s in range(A):
-        for d in (1, -1):
-            k = a - s * d
-
-            @pl.when((k >= 0) & (k < A) & has[d])
-            def _():
-                z_copy(x_ref, k, s, d).wait_send()
-
-    for k in range(A):
-        y_copy(x_ref, k, b).wait_send()
-        for bb in range(2):
-            c_copy(x_ref, k, bb, c).wait_send()
-
-
 def params(number):
     return pltpu.CompilerParams(collective_id=number, has_side_effects=True, vmem_limit_bytes=56 * 2**20)
-
-
-def gather(x, n, number):
-    A = n // 4
-    return pl.pallas_call(
-        functools.partial(gather_kernel, n),
-        out_shape=jax.ShapeDtypeStruct((n,) + x.shape, x.dtype),
-        in_specs=[pl.BlockSpec(memory_space=VM)],
-        out_specs=pl.BlockSpec(memory_space=VM),
-        scratch_shapes=[DMA((2 * A,)), DMA((A,)), DMA((A,)), DMA((A,)), DMA((2 * A,)), DMA((2 * A,))],
-        compiler_params=params(number),
-        name=f"gather_{number}",
-    )(x)
-
-
-def scatter_kernel(
-    n, left_ref, w_ref, out_ref, part, cbuf, ysend, yrecv, zsend, zright, zleft, cs, cr, ys, yr, zs, zr
-):
-    A = n // 4
-    me, a, b, c = place(n)
-    across, pair = index_of(a, 1 - b, c), index_of(a, b, 1 - c)
-    has = {1: a < A - 1, -1: a > 0}
-    toward = {1: me + 4, -1: me - 4}
-    landing = {1: zright, -1: zleft}
-    rows, width = out_ref.shape
-    for d in (1, -1):
-
-        @pl.when(has[d])
-        def _():
-            greet(toward[d])
-
-    greet(across)
-    greet(pair)
-    pl.semaphore_wait(
-        pltpu.get_barrier_semaphore(), 2 + has[1].astype(jnp.int32) + has[-1].astype(jnp.int32)
-    )
-
-    def near_last(visit):
-        for s in range(A - 1, -1, -1):
-            for d in (1, -1) if s else (1,):
-                k = a + s * d
-
-                @pl.when((k >= 0) & (k < A))
-                def _():
-                    visit(s, d, k)
-
-    def multiply(group, bb, cc):
-        left = jnp.concatenate([left_ref[index_of(k, bb, cc)] for k in range(A)], axis=0)
-        tile = min(width, 1024)
-
-        def columns(t, carry):
-            at = pl.ds(pl.multiple_of(t * tile, tile), tile)
-            found = jnp.dot(left, w_ref[:, at], preferred_element_type=jnp.float32)
-            part[group, :, :, at] = found.reshape(A, rows, tile)
-            return carry
-
-        lax.fori_loop(0, width // tile, columns, 0)
-
-    def c_copy(group, k, bb):
-        slot = bb * A + k
-        return remote(part.at[group, k], cbuf.at[slot], cs.at[slot], cr.at[slot], pair)
-
-    def y_copy(k):
-        return remote(ysend.at[k], yrecv.at[k], ys.at[k], yr.at[k], across)
-
-    def z_copy(k, d):
-        row = 0 if d == 1 else A
-        return remote(zsend.at[k], landing[d].at[k], zs.at[k], zr.at[row + k], toward[d])
-
-    def z_arrival(k, d):
-        row = 0 if d == 1 else A
-        return remote(zsend.at[k], landing[d].at[k], zs.at[k], zr.at[row + k], toward[-d])
-
-    multiply(0, 1 - b, 1 - c)
-    near_last(lambda s, d, k: c_copy(0, k, 1 - b).start())
-    multiply(1, 1 - b, c)
-
-    def send_across(s, d, k):
-        c_copy(0, k, 1 - b).wait_recv()
-        ysend[k] = (part[1, k] + cbuf[(1 - b) * A + k]).astype(jnp.bfloat16)
-        y_copy(k).start()
-
-    near_last(send_across)
-    multiply(2, b, 1 - c)
-    near_last(lambda s, d, k: c_copy(2, k, b).start())
-    multiply(3, b, c)
-
-    def pass_on(s, d, k):
-        c_copy(2, k, b).wait_recv()
-        y_copy(k).wait_recv()
-        part[3, k] = part[3, k] + cbuf[b * A + k] + yrecv[k].astype(jnp.float32)
-        for came in (d,) if s else (1, -1):
-
-            @pl.when(has[-came])
-            def _():
-                z_arrival(k, came).wait_recv()
-                part[3, k] = part[3, k] + landing[came][k].astype(jnp.float32)
-
-        if s:
-            zsend[k] = part[3, k].astype(jnp.bfloat16)
-            z_copy(k, d).start()
-        else:
-            out_ref[...] = part[3, k]
-
-    near_last(pass_on)
-
-    def finish(s, d, k):
-        y_copy(k).wait_send()
-        if s:
-            z_copy(k, d).wait_send()
-        c_copy(0, k, 1 - b).wait_send()
-        c_copy(2, k, b).wait_send()
-
-    near_last(finish)
-
-
-def scatter(left, w, n, number):
-    A = n // 4
-    rows, depth = left.shape[0] // n, left.shape[1]
-    block = (rows, w.shape[1])
-    half = jnp.bfloat16
-    return pl.pallas_call(
-        functools.partial(scatter_kernel, n),
-        out_shape=jax.ShapeDtypeStruct(block, jnp.float32),
-        in_specs=[pl.BlockSpec(memory_space=VM)] * 2,
-        out_specs=pl.BlockSpec(memory_space=VM),
-        scratch_shapes=[VM((4, A) + block, jnp.float32), VM((2 * A,) + block, jnp.float32)]
-        + [VM((A,) + block, half)] * 5
-        + [DMA((2 * A,)), DMA((2 * A,)), DMA((A,)), DMA((A,)), DMA((A,)), DMA((2 * A,))],
-        compiler_params=params(number),
-        name=f"scatter_{number}",
-    )(left.reshape(n, rows, depth), w)
 
 
 def pieces_of(n, width):
@@ -704,6 +483,247 @@
     return context
 
 
+def far_first(A, a):
+    low, high = 0, A - 1
+    found = []
+    for _ in range(A):
+        left = (a - low > high - a).astype(jnp.int32)
+        found.append(high + left * (low - high))
+        low, high = low + left, high - 1 + left
+    return found
+
+
+def feed_kernel(
+    n, x_ref, gain_ref, gate_ref, up_ref, down_ref, out_ref,
+    xs, w_gate, w_up, w_down, gates, ups, act, part, cbuf, ysend, yrecv, zsend, zland,
+    local, zs, zr, ys, yr, cs, cr, gs, gr, hs, hr, ts, tr,
+):
+    A = n // 4
+    me, a, b, c = place(n)
+    across, pair = index_of(a, 1 - b, c), index_of(a, b, 1 - c)
+    has, toward = neighbours(n)
+    P, W = xs.shape[0], xs.shape[-1]
+    rows = x_ref.shape[0]
+    greet_along(has, toward)
+    greet(across)
+    greet(pair)
+    loads = [
+        pltpu.make_async_copy(src, dst, local.at[i])
+        for i, (src, dst) in enumerate(((gate_ref, w_gate), (up_ref, w_up), (down_ref, w_down)))
+    ]
+    for load in loads:
+        load.start()
+    values = x_ref[...].astype(jnp.float32)
+    scale = lax.rsqrt(jnp.mean(values * values, axis=-1, keepdims=True) + epsilon)
+    for p in range(P):
+        at = slice(p * W, (p + 1) * W)
+        xs[p, b, c, a] = (values[:, at] * scale * gain_ref[:, at]).astype(jnp.bfloat16)
+    await_greetings(has, 2)
+
+    def z_copy(k, p, s, d):
+        block = xs.at[p, b, c, k]
+        return remote(block, block, zs.at[(0 if d == 1 else A) + s, p], zr.at[k, p], toward[d])
+
+    def y_copy(k, p, bb):
+        block = xs.at[p, bb, c, k]
+        return remote(block, block, ys.at[k, p], yr.at[k, p], across)
+
+    def c_copy(k, p, bb, cc):
+        block = xs.at[p, bb, cc, k]
+        return remote(block, block, cs.at[bb * A + k, p], cr.at[bb * A + k, p], pair)
+
+    for p in range(P):
+        for d in (1, -1):
+
+            @pl.when(has[d])
+            def _():
+                z_copy(a, p, 0, d).start()
+
+        y_copy(a, p, b).start()
+    for p in range(P):
+        c_copy(a, p, b, c).start()
+
+    def pass_on(s, p):
+        for d in (1, -1) if s else (1,):
+            k = a - s * d
+
+            @pl.when((k >= 0) & (k < A))
+            def _():
+                y_copy(k, p, 1 - b).wait_recv()
+                c_copy(k, p, 1 - b, c).start()
+
+    for s in range(1, A):
+        for p in range(P):
+            for d in (1, -1):
+                k = a - s * d
+
+                @pl.when((k >= 0) & (k < A))
+                def _():
+                    block = xs.at[p, b, c, k]
+                    remote(block, block, zs.at[0, p], zr.at[k, p], toward[-d]).wait_recv()
+
+                    @pl.when(has[d])
+                    def _():
+                        z_copy(k, p, s, d).start()
+
+                    y_copy(k, p, b).start()
+                    c_copy(k, p, b, c).start()
+
+            if s > 1:
+                pass_on(s - 2, p)
+    for p in range(P):
+        pass_on(A - 2, p)
+    for load in loads:
+        load.wait()
+
+    def contract(p):
+        for bb in range(2):
+            for k in range(A):
+                c_copy(k, p, bb, 1 - c).wait_recv()
+        left = xs[p].reshape(n * rows, W)
+        for w, sums in ((w_gate, gates), (w_up, ups)):
+            found = jnp.dot(left, w[p * W : (p + 1) * W, :], preferred_element_type=jnp.float32)
+            sums[...] = found if p == 0 else sums[...] + found
+
+    for p in range(P):
+        pass_on(A - 1, p)
+        if p:
+            contract(p - 1)
+    contract(P - 1)
+    for p in range(P):
+        for s in range(A):
+            for d in (1, -1):
+                k = a - s * d
+
+                @pl.when((k >= 0) & (k < A) & has[d])
+                def _():
+                    z_copy(k, p, s, d).wait_send()
+
+        for k in range(A):
+            y_copy(k, p, b).wait_send()
+            for bb in range(2):
+                c_copy(k, p, bb, c).wait_send()
+
+    tall = A * rows
+    for group in range(4):
+        at = slice(group * tall, (group + 1) * tall)
+        act[group] = (jax.nn.gelu(gates[at, :], approximate=True) * ups[at, :]).astype(jnp.bfloat16)
+
+    def multiply(i, p, bb, cc):
+        found = jnp.dot(act[2 * bb + cc], w_down[:, p * W : (p + 1) * W], preferred_element_type=jnp.float32)
+        part[i, p] = found.reshape(A, rows, W)
+
+    def g_copy(side, p):
+        return remote(part.at[2 * side, p], cbuf.at[side, p], gs.at[side, p], gr.at[side, p], pair)
+
+    def h_copy(k, p):
+        return remote(ysend.at[p, k], yrecv.at[p, k], hs.at[k, p], hr.at[k, p], across)
+
+    def t_copy(k, p, right):
+        return remote(
+            zsend.at[p, k], zland.at[right, p, k], ts.at[k, p], tr.at[right, k, p], me + 8 * right - 4
+        )
+
+    def t_arrival(k, p, right):
+        return remote(
+            zsend.at[p, k], zland.at[right, p, k], ts.at[k, p], tr.at[right, k, p], me - 8 * right + 4
+        )
+
+    order = far_first(A, a)
+    for t, k in enumerate(order):
+        for p in range(P):
+            if t == 0:
+                if p == 0:
+                    multiply(0, p, 1 - b, 1 - c)
+                    g_copy(0, p).start()
+                    multiply(1, p, 1 - b, c)
+                if p + 1 < P:
+                    multiply(0, p + 1, 1 - b, 1 - c)
+                    g_copy(0, p + 1).start()
+                g_copy(0, p).wait_recv()
+            ysend[p, k] = (part[1, p, k] + cbuf[0, p, k]).astype(jnp.bfloat16)
+            h_copy(k, p).start()
+            if t == 0 and p + 1 < P:
+                multiply(1, p + 1, 1 - b, c)
+    for p in range(P):
+        multiply(2, p, b, 1 - c)
+        g_copy(1, p).start()
+    for p in range(P):
+        multiply(3, p, b, c)
+    for t, k in enumerate(order):
+        right = (k > a).astype(jnp.int32)
+        for p in range(P):
+            if t == 0:
+                g_copy(1, p).wait_recv()
+            h_copy(k, p).wait_recv()
+            part[3, p, k] = part[3, p, k] + cbuf[1, p, k] + yrecv[p, k].astype(jnp.float32)
+            if t < A - 1:
+                comes = ((right == 1) & (a > 0)) | ((right == 0) & (a < A - 1))
+
+                @pl.when(comes)
+                def _():
+                    t_arrival(k, p, right).wait_recv()
+                    part[3, p, k] = part[3, p, k] + zland[right, p, k].astype(jnp.float32)
+
+                zsend[p, k] = part[3, p, k].astype(jnp.bfloat16)
+                t_copy(k, p, right).start()
+            else:
+                for came in (1, -1):
+
+                    @pl.when(has[-came])
+                    def _():
+                        side = (came + 1) // 2
+                        t_arrival(k, p, side).wait_recv()
+                        part[3, p, k] = part[3, p, k] + zland[side, p, k].astype(jnp.float32)
+
+                at = slice(p * W, (p + 1) * W)
+                out_ref[:, at] = (x_ref[:, at].astype(jnp.float32) + part[3, p, k]).astype(jnp.bfloat16)
+
+    for t, k in enumerate(order):
+        right = (k > a).astype(jnp.int32)
+        for p in range(P):
+            h_copy(k, p).wait_send()
+            if t < A - 1:
+                t_copy(k, p, right).wait_send()
+    for p in range(P):
+        g_copy(0, p).wait_send()
+        g_copy(1, p).wait_send()
+
+
+def feed(residual, gain, w_gate, w_up, w_down, n, number):
+    A = n // 4
+    rows, width = residual.shape
+    hidden_units = w_gate.shape[1]
+    P = pieces_of(n, width)
+    W = width // P
+    half, full = jnp.bfloat16, jnp.float32
+    return pl.pallas_call(
+        functools.partial(feed_kernel, n),
+        out_shape=jax.ShapeDtypeStruct((rows, width), half),
+        in_specs=[pl.BlockSpec(memory_space=m) for m in (VM, VM, pl.ANY, pl.ANY, pl.ANY)],
+        out_specs=pl.BlockSpec(memory_space=VM),
+        scratch_shapes=[
+            VM((P, 2, 2, A, rows, W), half),
+            VM(w_gate.shape, half),
+            VM(w_up.shape, half),
+            VM(w_down.shape, half),
+            VM((n * rows, hidden_units), full),
+            VM((n * rows, hidden_units), full),
+            VM((4, A * rows, hidden_units), half),
+            VM((4, P, A, rows, W), full),
+            VM((2, P, A, rows, W), full),
+        ]
+        + [VM((P, A, rows, W), half)] * 3
+        + [VM((2, P, A, rows, W), half)]
+        + [
+            DMA((3,)), DMA((2 * A, P)), DMA((A, P)), DMA((A, P)), DMA((A, P)), DMA((2 * A, P)), DMA((2 * A, P)),
+            DMA((2, P)), DMA((2, P)), DMA((A, P)), DMA((A, P)), DMA((A, P)), DMA((2, A, P)),
+        ],
+        compiler_params=params(number),
+        name=f"feed_{number}",
+    )(residual, gain[None, :], w_gate, w_up, w_down)
+
+
 def per_device(
     n,
     hidden,
@@ -722,12 +742,7 @@
     query, plane = make_query(hidden, norm_gain_attn, w_query, w_out, n, 0)
     context = attend(query.reshape(-1, PAD), entering_kv, cached_kv, enc_lengths, n, 1)
     residual = project(context.reshape(n, rows, PAD), hidden, w_out, plane, n, 3)
-    portion = gather(normalize(residual, norm_gain_ffn), n, 4).reshape(-1, width)
-    gate = jnp.dot(portion, w_gate, preferred_element_type=jnp.float32)
-    upward = jnp.dot(portion, w_up, preferred_element_type=jnp.float32)
-    activated = (jax.nn.gelu(gate, approximate=True) * upward).astype(jnp.bfloat16)
-    feed_out = scatter(activated, w_down, n, 5)
-    return (residual.astype(jnp.float32) + feed_out).astype(jnp.bfloat16)
+    return feed(residual, norm_gain_ffn, w_gate, w_up, w_down, n, 4)
 
 
 def solution(mesh):

time: 185 us -> 164 us (0.89)
  matrix products: 12.4 us -> 0 us
  Pallas kernels: 165 us -> 160 us
  other arithmetic: 6.1 us -> 1.4 us
    dot_general x2 -> x0, matrix products: 12.4 us -> none  [the longest x1 6.89 us: per_device(): upward = jnp.dot(portion, w_up, preferred_element_type=jnp.float32)]
    pallas_call x2 -> x1, Pallas kernels: 68.4 us -> 63.5 us  [feed(): pl.pallas_call(functools.partial(feed_kernel, n), out_shape=jax.ShapeDtyp...]
    convert_element_type x2 -> x0, other arithmetic: 3.58 us -> none  [the longest x1 1.79 us: per_device(): return (residual.astype(jnp.float32) + feed_out).astype(jnp.bfloat16)]
where the time goes in v2:
time: 164 us
  Pallas kernels  160 us (98%)
  local copies, waits for them, and re-layouts  2.43 us (1%)
    pallas_call x1, Pallas kernels, feed(): pl.pallas_call(functools.partial(feed_kernel, n), out_shape=jax.ShapeDtyp...  63.5 us
    pallas_call x1, Pallas kernels, attend(): pl.pallas_call(functools.partial(attend_kernel, n), out_shape=jax.ShapeDt...  39.4 us
    pallas_call x1, Pallas kernels, make_query(): pl.pallas_call(functools.partial(query_kernel, n), out_shape=[jax.ShapeDt...  32.8 us
    pallas_call x1, Pallas kernels, project(): pl.pallas_call(functools.partial(project_kernel, n), out_shape=jax.ShapeD...  24.3 us

profile of v2, /device:TPU:0, one launch (start us, length us, event | category | flops | bytes accessed | tf_op | source)
XLA Modules:
  0.0 163.8 jit_solution(13890254207532221738)
XLA Ops:
  0.0 0.8 slice_bitcast_fusion
  0.8 0.7 compare_convert_fusion.1.mask_ref
  1.4 0.7 compare_convert_fusion.cached_mask_ref
  2.2 32.8 %query_0.1 = (bf16[16,32,128]{2,1,0:T(8,128)(2,1)}, bf16[3,64,4096]{2,1,0:T(8,128)(2,1)}) custom-call(bf16[32,4096]{1,0:T(8,128)(2,1)} %hidden_ref.1, f32[1,4096]{1,0:T(1,128)} %bitcast.15, bf16[64,4096]{1,0:T(8,128)(2,1)} %bitcast.11, bf16[64,4096]{1,0:T(8,128)(2,1)} %wo_ref.3), custom_call_target="tpu_custom_call" | custom-call | tf_op jit(solution)/shard_map/query_0/pallas_call | solution.py:181
  34.9 39.4 %attend_1.1 = bf16[512,128]{1,0:T(8,128)(2,1)} custom-call(bf16[512,128]{1,0:T(8,128)(2,1)} %bitcast.12, bf16[8,128,2048]{2,1,0:T(8,128)(2,1)} %kv_ref.1, bf16[8,2048,128]{2,1,0:T(8,128)(2,1)} %cached_ref.1, f32[8,1,128]{2,1,0:T(1,128)} %compare_convert_fusion.1.mask_ref, f32[8,1,2048]{2,1,0:T(1,128)} %compare_convert_fusion.cached_mask_ref), custom_call_target="tpu_custom_call" | custom-call | tf_op jit(solution)/shard_map/attend_1/pallas_call | solution.py:459
  74.4 24.3 %project_3.1.x_ref = bf16[32,4096]{1,0:T(8,128)(2,1)} custom-call(bf16[16,32,128]{2,1,0:T(8,128)(2,1)} %bitcast.10, bf16[32,4096]{1,0:T(8,128)(2,1)} %hidden_ref.1, bf16[64,4096]{1,0:T(8,128)(2,1)} %wo_ref.3, bf16[3,64,4096]{2,1,0:T(8,128)(2,1)} %get-tuple-element.8.plane_ref), custom_call_target="tpu_custom_call" | custom-call | tf_op jit(solution)/shard_map/project_3/pallas_call | solution.py:292
  98.7 63.5 %feed_4.1 = bf16[32,4096]{1,0:T(8,128)(2,1)} custom-call(bf16[32,4096]{1,0:T(8,128)(2,1)} %project_3.1.x_ref, f32[1,4096]{1,0:T(1,128)} %bitcast.13, bf16[4096,640]{1,0:T(8,128)(2,1)} %gate_ref.1, bf16[4096,640]{1,0:T(8,128)(2,1)} %up_ref.1, bf16[640,4096]{1,0:T(8,128)(2,1)} %down_ref.1), custom_call_target="tpu_custom_call" | custom-call | tf_op jit(solution)/shard_map/feed_4/pallas_call | solution.py:700
  162.1 1.7 %copy.14 = bf16[32,4096]{1,0:T(8,128)(2,1)} copy(bf16[32,4096]{1,0:T(8,128)(2,1)} %feed_4.1) | data formatting | bytes 524288
  (2 shorter events, 0.0 us)

commit v3 on v2

--- a/solution.py
+++ b/solution.py
@@ -67,26 +67,33 @@
 
 
 def query_kernel(
-    n, x_ref, gain_ref, wq_ref, wo_ref, q_ref, plane_ref,
-    xs, w2, q_send, q_recv, local, zs, zr, cs, cr, ws, wr, ps, pr,
+    n, groups, x_ref, gain_ref, wq_ref, wo_ref, q_ref, plane_ref,
+    xs, w2, local, zs, zr, cs, cr, ys, yr, gs, gr, ps, pr,
 ):
     A = n // 4
     me, a, b, c = place(n)
+    mine = lax.axis_index("groups")
     across, pair = index_of(a, 1 - b, c), index_of(a, b, 1 - c)
     has, toward = neighbours(n)
     P, W = xs.shape[0], xs.shape[-1]
     rows = x_ref.shape[0]
+    share = DH // groups
+    twins = [lax.rem(mine + i, groups) for i in range(1, groups)]
     greet_along(has, toward)
     greet(across)
     greet(pair)
-    load_w = pltpu.make_async_copy(wq_ref, w2.at[0], local.at[0])
+    for twin in twins:
+        pl.semaphore_signal(
+            pltpu.get_barrier_semaphore(), inc=1, device_id={"groups": twin, "mp": me}, device_id_type=MESH
+        )
+    load_w = pltpu.make_async_copy(wq_ref, w2.at[b], local.at[0])
     load_w.start()
     values = x_ref[...].astype(jnp.float32)
     scale = lax.rsqrt(jnp.mean(values * values, axis=-1, keepdims=True) + epsilon)
     for p in range(P):
         part = slice(p * W, (p + 1) * W)
         xs[p, a, c] = (values[:, part] * scale * gain_ref[:, part]).astype(jnp.bfloat16)
-    await_greetings(has, 2)
+    await_greetings(has, 1 + groups)
 
     def z_copy(k, p, s, d):
         row = 0 if d == 1 else A
@@ -95,11 +102,29 @@
     def c_copy(k, p, cc):
         return remote(xs.at[p, k, cc], xs.at[p, k, cc], cs.at[k, p], cr.at[k, p], pair)
 
-    wq_copy = remote(wq_ref, w2.at[1], ws.at[0], wr.at[0], across)
-    q_copy = remote(q_send, q_recv, ws.at[1], wr.at[1], across)
+    def strip(part):
+        return pl.ds(pl.multiple_of(part * share, share), share)
+
+    def landing(which, bb, part):
+        return w2.at[bb, strip(part)] if which == 0 else plane_ref.at[1, strip(part)]
+
+    def y_copy(which):
+        source = (wq_ref, wo_ref)[which].at[strip(mine)]
+        return remote(source, landing(which, b, mine), ys.at[which], yr.at[which], across)
+
+    def y_arrival(which):
+        spot = landing(which, 1 - b, mine)
+        return remote(spot, spot, ys.at[which], yr.at[which], across)
+
+    def g_copy(which, part, to):
+        spot = landing(which, 1 - b, part)
+        return pltpu.make_async_remote_copy(
+            src_ref=spot, dst_ref=spot, send_sem=gs.at[which, to], recv_sem=gr.at[which, part],
+            device_id={"groups": to, "mp": me}, device_id_type=MESH,
+        )
+
     plane_pair = remote(wo_ref, plane_ref.at[0], ps.at[0], pr.at[0], pair)
-    plane_across = remote(wo_ref, plane_ref.at[1], ps.at[1], pr.at[1], across)
-    plane_diagonal = remote(plane_ref.at[1], plane_ref.at[2], ps.at[2], pr.at[2], pair)
+    plane_diagonal = remote(plane_ref.at[1], plane_ref.at[2], ps.at[1], pr.at[1], pair)
     for p in range(P):
         for d in (1, -1):
 
@@ -107,8 +132,8 @@
             def _():
                 z_copy(a, p, 0, d).start()
 
-    wq_copy.start()
-    plane_across.start()
+    for which in range(2):
+        y_copy(which).start()
     for p in range(P):
         c_copy(a, p, c).start()
     plane_pair.start()
@@ -127,26 +152,24 @@
 
                     c_copy(k, p, c).start()
 
+        if s < 3:
+            y_arrival(s - 1).wait_recv()
+            for twin in twins:
+                g_copy(s - 1, mine, twin).start()
+    for which in range(2):
+        for twin in twins:
+            g_copy(which, twin, mine).wait_recv()
+    plane_diagonal.start()
     load_w.wait()
-    wq_copy.wait_recv()
-    for k in range(A):
-        for p in range(P):
+    total = jnp.zeros((2 * A * rows, PAD), jnp.float32)
+    for p in range(P):
+        for k in range(A):
             c_copy(k, p, 1 - c).wait_recv()
-    total = jnp.zeros((2 * A * rows, PAD), jnp.float32)
-    for p in range(P):
         total = total + lax.dot_general(
             xs[p].reshape(2 * A * rows, W), w2[:, :, p * W : (p + 1) * W].reshape(PAD, W),
             (((1,), (1,)), ((), ())), preferred_element_type=jnp.float32,
         )
-    q_send[...] = total.astype(jnp.bfloat16)
-    low = lax.broadcasted_iota(jnp.int32, (2 * A * rows, PAD), 1) < DH
-    own = jnp.where(low, total, 0.0).astype(jnp.bfloat16).reshape(2 * A, rows, PAD)
-    for k in range(A):
-        for cc in range(2):
-            q_ref[index_of(k, b, cc)] = own[2 * k + cc]
-    q_copy.start()
-    plane_across.wait_recv()
-    plane_diagonal.start()
+    q_ref[...] = total.astype(jnp.bfloat16).reshape(2 * A, rows, PAD)
     for s in range(A):
         for d in (1, -1):
             k = a - s * d
@@ -159,29 +182,25 @@
     for k in range(A):
         for p in range(P):
             c_copy(k, p, c).wait_send()
-    q_copy.wait_recv()
-    came = pltpu.roll(q_recv[...].astype(jnp.float32), DH, 1)
-    came = jnp.where(low, came, 0.0).astype(jnp.bfloat16).reshape(2 * A, rows, PAD)
-    for k in range(A):
-        for cc in range(2):
-            q_ref[index_of(k, 1 - b, cc)] = came[2 * k + cc]
-    wq_copy.wait_send()
-    q_copy.wait_send()
-    plane_across.wait_send()
+    for which in range(2):
+        y_copy(which).wait_send()
+        for twin in twins:
+            g_copy(which, mine, twin).wait_send()
     plane_pair.wait()
     plane_diagonal.wait()
 
 
-def make_query(hidden, gain, w_query, w_out, n, number):
+def make_query(hidden, gain, w_query, w_out, n, groups, number):
     A = n // 4
+    assert A > 2 and DH % groups == 0
     rows, width = hidden.shape
     P = pieces_of(n, width)
     W = width // P
     half = jnp.bfloat16
     return pl.pallas_call(
-        functools.partial(query_kernel, n),
+        functools.partial(query_kernel, n, groups),
         out_shape=[
-            jax.ShapeDtypeStruct((n, rows, PAD), half),
+            jax.ShapeDtypeStruct((2 * A, rows, PAD), half),
             jax.ShapeDtypeStruct((3,) + w_out.shape, half),
         ],
         in_specs=[pl.BlockSpec(memory_space=m) for m in (VM, VM, pl.ANY, pl.ANY)],
@@ -189,10 +208,8 @@
         scratch_shapes=[
             VM((P, A, 2, rows, W), half),
             VM((2, DH, width), half),
-            VM((2 * A * rows, PAD), half),
-            VM((2 * A * rows, PAD), half),
             DMA((1,)), DMA((2 * A, P)), DMA((A, P)), DMA((A, P)), DMA((A, P)),
-            DMA((2,)), DMA((2,)), DMA((3,)), DMA((3,)),
+            DMA((2,)), DMA((2,)), DMA((2, groups)), DMA((2, groups)), DMA((2,)), DMA((2,)),
         ],
         compiler_params=params(number),
         name=f"query_{number}",
@@ -308,12 +325,17 @@
 
 
 def attend_kernel(
-    n, own_ref, kv_ref, cached_ref, mask_ref, cached_mask_ref, out_ref,
-    q_ref, q_all, kv, cached, scores, chances, o_send, o_recv, st_send, st_recv, local, qs, qr, os, orr, ss, sr,
+    n, lengths_ref, q_ref, kv_ref, cached_ref, out_ref,
+    q_all, q_cached, kv, cached, scores, chances, o_send, o_recv, stats, st_send, st_recv,
+    local, qzs, qzr, qys, qyr, qcs, qcr, os, orr, ss, sr,
 ):
-    me = lax.axis_index("mp")
+    A = n // 4
+    me, a, b, c = place(n)
+    across, pair = index_of(a, 1 - b, c), index_of(a, b, 1 - c)
     requests, positions, width = kv.shape
     pairs, heads = requests // 2, width // PAD
+    rows = q_ref.shape[1]
+    length = cached.shape[1]
     load_cached = pltpu.make_async_copy(cached_ref, cached, local.at[0])
     load_kv = pltpu.make_async_copy(kv_ref, kv, local.at[1])
     load_cached.start()
@@ -322,60 +344,109 @@
     others = [lax.rem(me + s, n) for s in order]
     for other in others:
         greet(other)
-    for step in range(pairs):
-        even, odd = (
-            own_ref[(2 * step + i) * QLEN : (2 * step + i + 1) * QLEN, :].astype(jnp.float32) for i in range(2)
-        )
-        q_ref[step * QLEN : (step + 1) * QLEN, :] = (even + pltpu.roll(odd, DH, 1)).astype(jnp.bfloat16)
+    columns = [lax.rem(a + s, A) for s in range(1, A)]
+    entering, flying = pl.ds(0, A), pl.ds(A, A)
+    q_all[a, c, b] = q_ref[:A]
+    q_cached[b] = q_ref[A:]
+    stats[...] = jnp.zeros_like(stats)
     pl.semaphore_wait(pltpu.get_barrier_semaphore(), n - 1)
 
-    def q_copy(other, spot):
-        return remote(q_ref, q_all.at[spot], qs.at[other], qr.at[spot], other)
+    def qz_copy(to, k):
+        return remote(q_ref.at[entering], q_all.at[k, c, b], qzs.at[to], qzr.at[k], index_of(to, b, c))
+
+    def qy_copy(k, bb, src=None):
+        spot = q_all.at[k, c, bb]
+        return remote(spot if src is None else src, spot, qys.at[k], qyr.at[k], across)
+
+    def qc_copy(k, bb, cc, src=None):
+        spot = q_all.at[k, cc, bb]
+        return remote(spot if src is None else src, spot, qcs.at[bb * A + k], qcr.at[bb * A + k], pair)
+
+    def cached_copy(bb):
+        return remote(q_ref.at[flying], q_cached.at[bb], qys.at[A], qyr.at[A], across)
 
     def o_copy(other, spot, step):
-        rows = pl.ds(pl.multiple_of(step * QLEN, QLEN), QLEN)
+        at = pl.ds(pl.multiple_of(step * QLEN, QLEN), QLEN)
         return remote(
-            o_send.at[other, rows], o_recv.at[spot, rows], os.at[step, other], orr.at[step, spot], other
+            o_send.at[other, at], o_recv.at[spot, at], os.at[step, other], orr.at[step, spot], other
         )
 
     def st_copy(other, spot):
         return remote(st_send.at[other], st_recv.at[spot], ss.at[other], sr.at[spot], other)
 
-    for other in others:
-        q_copy(other, me).start()
-    q_all[me] = q_ref[...]
+    for k in columns:
+        qz_copy(k, a).start()
+    qy_copy(a, b, q_ref.at[entering]).start()
+    cached_copy(b).start()
+    qc_copy(a, b, c, q_ref.at[entering]).start()
     lane = lax.broadcasted_iota(jnp.int32, (QLEN, PAD), 1)
-    load_cached.wait()
-
-    def cached_request(r, carry):
+    low = lane < DH
+
+    def request_of(r, block):
+        per = QLEN // rows
+        parts = []
+        for i in range(per):
+            spot = r * per + i
+            parts.append(block((spot // 2) % 2, (spot // 4) * 2 + spot % 2))
+        return parts[0] if per == 1 else jnp.concatenate(parts, axis=0)
+
+    def cached_request(r):
         to = pl.ds(pl.multiple_of((requests + r) * QLEN, QLEN), QLEN)
         block = cached[r]
+        query = request_of(r, lambda bb, spot: q_cached[bb, spot]).astype(jnp.float32)
+        query = jnp.where(b == 0, query, pltpu.roll(query, DH, 1))
         found = lax.dot_general(
-            own_ref[to, :], block, (((1,), (1,)), ((), ())), preferred_element_type=jnp.float32
+            jnp.where(low, query, 0.0).astype(jnp.bfloat16), block, (((1,), (1,)), ((), ())),
+            preferred_element_type=jnp.float32,
         )
-        usable = cached_mask_ref[r] > 0.5
+        usable = lax.broadcasted_iota(jnp.int32, (1, length), 1) < lengths_ref[1, r]
         masked = jnp.where(usable, found, -1e30)
-        exponent = jnp.where(usable, jnp.exp(masked - jnp.max(masked, axis=-1, keepdims=True)), 0.0)
-        weights = (exponent / jnp.sum(exponent, axis=-1, keepdims=True)).astype(jnp.bfloat16)
+        exponent = jnp.exp(masked - jnp.max(masked, axis=-1, keepdims=True))
+        inverse = 1.0 / jnp.sum(exponent, axis=-1, keepdims=True)
+        weights = (exponent * inverse).astype(jnp.bfloat16)
         out_ref[to, :] = jnp.dot(weights, block, preferred_element_type=jnp.float32).astype(jnp.bfloat16)
-        return carry
-
-    lax.fori_loop(0, requests, cached_request, 0)
-    st_send[...] = jnp.zeros_like(st_send)
+
+    def cached_requests(start, stop):
+        def two(i, carry):
+            cached_request(start + 2 * i)
+            cached_request(start + 2 * i + 1)
+            return carry
+
+        lax.fori_loop(0, (stop - start) // 2, two, 0)
+        if (stop - start) % 2:
+            cached_request(stop - 1)
+
+    for k in columns:
+        qz_copy(k, k).wait_recv()
+        qy_copy(k, b).start()
+        qc_copy(k, b, c).start()
+    cached_copy(1 - b).wait_recv()
+    load_cached.wait()
+    first, second = requests // 4, requests // 2
+    cached_requests(0, first)
+    qy_copy(a, 1 - b).wait_recv()
+    qc_copy(a, 1 - b, c).start()
+    for k in columns:
+        qy_copy(k, 1 - b).wait_recv()
+        qc_copy(k, 1 - b, c).start()
+    cached_requests(first, second)
     load_kv.wait()
-    for other in others:
-        q_copy(other, other).wait_recv()
+    for k in range(A):
+        for bb in range(2):
+            qc_copy(k, bb, 1 - c).wait_recv()
+    at_position = me * positions + lax.broadcasted_iota(jnp.int32, (1, positions), 1)
 
     def pair_step(step, carry):
-        rows = pl.ds(pl.multiple_of(step * QLEN, QLEN), QLEN)
-        low = lane < DH
+        at = pl.ds(pl.multiple_of(step * QLEN, QLEN), QLEN)
         nothing = jnp.zeros((QLEN, PAD), jnp.bfloat16)
         for i in range(2):
             for g in range(heads // 2):
                 two = []
-                for h in (2 * g, 2 * g + 1):
-                    packed = q_all[h, rows, :].astype(jnp.float32)
-                    packed = packed if i == 0 else pltpu.roll(packed, DH, 1)
+                for cc in range(2):
+                    packed = request_of(
+                        step * 2 + i, lambda bb, spot: q_all[g // 2, cc, bb, spot]
+                    ).astype(jnp.float32)
+                    packed = packed if g % 2 == 0 else pltpu.roll(packed, DH, 1)
                     two.append(jnp.where(low, packed, 0.0).astype(jnp.bfloat16))
                 spread = jnp.concatenate(
                     [
@@ -390,16 +461,15 @@
                 )
         for i in range(2):
             r = step * 2 + i
-            usable = mask_ref[r] > 0.5
-            masked = jnp.where(usable, scores[i], -1e30)
+            masked = jnp.where(at_position < lengths_ref[0, r], scores[i], -1e30)
             largest = jnp.max(masked, axis=-1, keepdims=True)
-            exponent = jnp.where(usable, jnp.exp(masked - largest), 0.0)
+            exponent = jnp.exp(masked - largest)
             total = jnp.sum(exponent, axis=-1, keepdims=True)
             chances[i] = exponent.astype(jnp.bfloat16)
-            st_send[...] = jnp.where(
+            stats[...] = jnp.where(
                 lane == r,
                 largest.reshape(heads, QLEN, 1),
-                jnp.where(lane == r + DH, total.reshape(heads, QLEN, 1), st_send[...]),
+                jnp.where(lane == r + requests, total.reshape(heads, QLEN, 1), stats[...]),
             )
         for g in range(heads // 2):
             found = [
@@ -411,76 +481,89 @@
             ]
             for e in range(2):
                 even, odd = (f[e * QLEN : (e + 1) * QLEN, e * PAD : (e + 1) * PAD] for f in found)
-                o_send[2 * g + e, rows, :] = jnp.where(low, pltpu.roll(odd, DH, 1), even).astype(jnp.bfloat16)
+                o_send[2 * g + e, at, :] = jnp.where(low, pltpu.roll(odd, DH, 1), even).astype(jnp.bfloat16)
         for other in others:
             o_copy(other, me, step).start()
         return carry
 
     lax.fori_loop(0, pairs, pair_step, 0)
+    parts = QLEN // 8
+    gap = PAD // parts
+    folded = stats[:, :8, :].reshape(heads * 8, PAD)
+    for g in range(1, parts):
+        folded = folded + pltpu.roll(stats[:, 8 * g : 8 * g + 8, :].reshape(heads * 8, PAD), g * gap, 1)
+    st_send[...] = folded.reshape(heads, 8, PAD)
     for other in others:
         st_copy(other, me).start()
     o_recv[me] = o_send[me]
     st_recv[me] = st_send[me]
+    cached_requests(second, requests)
     for other in others:
         st_copy(other, other).wait_recv()
     largest = st_recv[...]
     scale = jnp.exp(largest - jnp.max(largest, axis=0, keepdims=True))
     total = jnp.sum(
-        scale * pltpu.roll(largest.reshape(n * QLEN, PAD), DH, 1).reshape(n, QLEN, PAD), axis=0, keepdims=True
+        scale * pltpu.roll(largest.reshape(n * 8, PAD), PAD - requests, 1).reshape(n, 8, PAD), axis=0, keepdims=True
     )
     st_recv[...] = scale / jnp.where(total > 0.0, total, 1.0)
+    short = low[:8]
     for step in range(pairs):
         for other in others:
             o_copy(other, other, step).wait_recv()
         mixed = jnp.zeros((QLEN, PAD), jnp.float32)
         for d in range(n):
-            share = st_recv[d]
-            share = jnp.where(
-                lane < DH, share[:, 2 * step + 1 : 2 * step + 2], share[:, 2 * step : 2 * step + 1]
-            )
+            known = st_recv[d]
+            share = []
+            for g in range(parts):
+                lone = g * gap + 2 * step
+                share.append(jnp.where(short, known[:, lone + 1 : lone + 2], known[:, lone : lone + 1]))
+            share = jnp.concatenate(share, axis=0)
             mixed = mixed + share * o_recv[d, step * QLEN : (step + 1) * QLEN, :].astype(jnp.float32)
         out_ref[2 * step * QLEN : (2 * step + 1) * QLEN, :] = mixed.astype(jnp.bfloat16)
         out_ref[(2 * step + 1) * QLEN : (2 * step + 2) * QLEN, :] = pltpu.roll(mixed, DH, 1).astype(jnp.bfloat16)
+    for k in columns:
+        qz_copy(k, a).wait_send()
+    cached_copy(b).wait_send()
+    for k in range(A):
+        qy_copy(k, b).wait_send()
+        for bb in range(2):
+            qc_copy(k, bb, c).wait_send()
     for other in others:
-        q_copy(other, me).wait_send()
         st_copy(other, me).wait_send()
         for step in range(pairs):
             o_copy(other, me, step).wait_send()
 
 
 def attend(query, entering_kv, cached_kv, lengths, n, number):
+    A = n // 4
     requests, positions, width = entering_kv.shape
-    length = cached_kv.shape[1]
     pairs, heads = requests // 2, width // PAD
-    start = lax.axis_index("mp") * positions
-    usable = (start + jnp.arange(positions, dtype=jnp.int32))[None, :] < lengths[0][:, None]
-    cached_usable = jnp.arange(length, dtype=jnp.int32)[None, :] < lengths[1][:, None]
-    half_type = jnp.bfloat16
-    context = pl.pallas_call(
+    rows = query.shape[1]
+    assert heads == n and QLEN % rows == 0 and 8 * requests <= PAD
+    half, full = jnp.bfloat16, jnp.float32
+    return pl.pallas_call(
         functools.partial(attend_kernel, n),
-        out_shape=jax.ShapeDtypeStruct((2 * requests * QLEN, PAD), half_type),
-        in_specs=[pl.BlockSpec(memory_space=m) for m in (VM, pl.ANY, pl.ANY, VM, VM)],
+        out_shape=jax.ShapeDtypeStruct((2 * requests * QLEN, PAD), half),
+        in_specs=[pl.BlockSpec(memory_space=m) for m in (pltpu.SMEM, VM, pl.ANY, pl.ANY)],
         out_specs=pl.BlockSpec(memory_space=VM),
         scratch_shapes=[
-            VM((pairs * QLEN, PAD), half_type),
-            VM((n, pairs * QLEN, PAD), half_type),
-            VM(entering_kv.shape, half_type),
-            VM(cached_kv.shape, half_type),
-            VM((2, heads // 2, 2 * QLEN, positions), jnp.float32),
-            VM((2, heads // 2, 2 * QLEN, positions), half_type),
-            VM((n, pairs * QLEN, PAD), half_type),
-            VM((n, pairs * QLEN, PAD), half_type),
-            VM((n, QLEN, PAD), jnp.float32),
-            VM((n, QLEN, PAD), jnp.float32),
-            DMA((2,)), DMA((n,)), DMA((n,)), DMA((pairs, n)), DMA((pairs, n)), DMA((n,)), DMA((n,)),
+            VM((A, 2, 2, A, rows, PAD), half),
+            VM((2, A, rows, PAD), half),
+            VM(entering_kv.shape, half),
+            VM(cached_kv.shape, half),
+            VM((2, heads // 2, 2 * QLEN, positions), full),
+            VM((2, heads // 2, 2 * QLEN, positions), half),
+            VM((n, pairs * QLEN, PAD), half),
+            VM((n, pairs * QLEN, PAD), half),
+            VM((n, QLEN, PAD), full),
+            VM((n, 8, PAD), full),
+            VM((n, 8, PAD), full),
+            DMA((2,)), DMA((A,)), DMA((A,)), DMA((A + 1,)), DMA((A + 1,)), DMA((2 * A,)), DMA((2 * A,)),
+            DMA((pairs, n)), DMA((pairs, n)), DMA((n,)), DMA((n,)),
         ],
         compiler_params=params(number),
         name=f"attend_{number}",
-    )(
-        query, entering_kv, cached_kv,
-        usable.astype(jnp.float32)[:, None, :], cached_usable.astype(jnp.float32)[:, None, :],
-    )
-    return context
+    )(lengths, query, entering_kv, cached_kv)
 
 
 def far_first(A, a):
@@ -726,6 +809,7 @@
 
 def per_device(
     n,
+    groups,
     hidden,
     norm_gain_attn,
     w_query,
@@ -739,8 +823,8 @@
     w_down,
 ):
     rows, width = hidden.shape
-    query, plane = make_query(hidden, norm_gain_attn, w_query, w_out, n, 0)
-    context = attend(query.reshape(-1, PAD), entering_kv, cached_kv, enc_lengths, n, 1)
+    query, plane = make_query(hidden, norm_gain_attn, w_query, w_out, n, groups, 0)
+    context = attend(query, entering_kv, cached_kv, enc_lengths, n, 1)
     residual = project(context.reshape(n, rows, PAD), hidden, w_out, plane, n, 3)
     return feed(residual, norm_gain_ffn, w_gate, w_up, w_down, n, 4)
 
@@ -760,7 +844,7 @@
         P("mp", None),
     )
     return jax.shard_map(
-        functools.partial(per_device, mesh.shape["mp"]),
+        functools.partial(per_device, mesh.shape["mp"], mesh.shape["groups"]),
         mesh=mesh,
         in_specs=placed,
         out_specs=P(("groups", "mp"), None),

time: 164 us -> 152 us (0.927)
  Pallas kernels: 160 us -> 150 us
    pallas_call x1, Pallas kernels: 39.4 us -> 33.4 us  [attend(): pl.pallas_call(functools.partial(attend_kernel, n), out_shape=jax.ShapeDt...]
    pallas_call x1, Pallas kernels: 32.8 us -> 28.1 us  [make_query(): pl.pallas_call(functools.partial(query_kernel, n, groups), out_shape=[jax...]
where the time goes in v3:
time: 152 us
  Pallas kernels  150 us (99%)
  local copies, waits for them, and re-layouts  1.67 us (1%)
    pallas_call x1, Pallas kernels, feed(): pl.pallas_call(functools.partial(feed_kernel, n), out_shape=jax.ShapeDtyp...  64.4 us
    pallas_call x1, Pallas kernels, attend(): pl.pallas_call(functools.partial(attend_kernel, n), out_shape=jax.ShapeDt...  33.4 us
    pallas_call x1, Pallas kernels, make_query(): pl.pallas_call(functools.partial(query_kernel, n, groups), out_shape=[jax...  28.1 us
    pallas_call x1, Pallas kernels, project(): pl.pallas_call(functools.partial(project_kernel, n), out_shape=jax.ShapeD...  24.1 us

profile of v3, /device:TPU:0, one launch (start us, length us, event | category | flops | bytes accessed | tf_op | source)
XLA Modules:
  0.0 151.6 jit_solution(15236697883436926837)
XLA Ops:
  0.0 28.1 %query_0.1 = (bf16[8,32,128]{2,1,0:T(8,128)(2,1)}, bf16[3,64,4096]{2,1,0:T(8,128)(2,1)}) custom-call(bf16[32,4096]{1,0:T(8,128)(2,1)} %hidden_ref.1, f32[1,4096]{1,0:T(1,128)} %bitcast.7, bf16[64,4096]{1,0:T(8,128)(2,1)} %bitcast.5, bf16[64,4096]{1,0:T(8,128)(2,1)} %wo_ref.3), custom_call_target="tpu_custom_call" | custom-call | tf_op jit(solution)/shard_map/query_0/pallas_call | solution.py:200
  28.1 33.4 %attend_1.1 = bf16[512,128]{1,0:T(8,128)(2,1)} custom-call(s32[2,8]{1,0:T(2,128)} %lengths_ref.1, bf16[8,32,128]{2,1,0:T(8,128)(2,1)} %get-tuple-element.7.q_ref, bf16[8,128,2048]{2,1,0:T(8,128)(2,1)} %kv_ref.1, bf16[8,2048,128]{2,1,0:T(8,128)(2,1)} %cached_ref.1), custom_call_target="tpu_custom_call" | custom-call | tf_op jit(solution)/shard_map/attend_1/pallas_call | solution.py:544
  61.5 24.1 %project_3.1.x_ref = bf16[32,4096]{1,0:T(8,128)(2,1)} custom-call(bf16[16,32,128]{2,1,0:T(8,128)(2,1)} %bitcast.4, bf16[32,4096]{1,0:T(8,128)(2,1)} %hidden_ref.1, bf16[64,4096]{1,0:T(8,128)(2,1)} %wo_ref.3, bf16[3,64,4096]{2,1,0:T(8,128)(2,1)} %get-tuple-element.8.plane_ref), custom_call_target="tpu_custom_call" | custom-call | tf_op jit(solution)/shard_map/project_3/pallas_call | solution.py:309
  85.6 64.4 %feed_4.1 = bf16[32,4096]{1,0:T(8,128)(2,1)} custom-call(bf16[32,4096]{1,0:T(8,128)(2,1)} %project_3.1.x_ref, f32[1,4096]{1,0:T(1,128)} %bitcast.6, bf16[4096,640]{1,0:T(8,128)(2,1)} %gate_ref.1, bf16[4096,640]{1,0:T(8,128)(2,1)} %up_ref.1, bf16[640,4096]{1,0:T(8,128)(2,1)} %down_ref.1), custom_call_target="tpu_custom_call" | custom-call | tf_op jit(solution)/shard_map/feed_4/pallas_call | solution.py:783
  150.0 1.7 %copy.13 = bf16[32,4096]{1,0:T(8,128)(2,1)} copy(bf16[32,4096]{1,0:T(8,128)(2,1)} %feed_4.1) | data formatting | bytes 524288

commit v4 on v3

--- a/solution.py
+++ b/solution.py
@@ -36,10 +36,6 @@
     pl.semaphore_signal(pltpu.get_barrier_semaphore(), inc=1, device_id={"mp": to}, device_id_type=MESH)
 
 
-def params(number):
-    return pltpu.CompilerParams(collective_id=number, has_side_effects=True, vmem_limit_bytes=56 * 2**20)
-
-
 def pieces_of(n, width):
     return max(1, min(4, 16 // (n // 4), width // 128))
 
@@ -52,23 +48,8 @@
     return has, toward
 
 
-def greet_along(has, toward):
-    for d in (1, -1):
-
-        @pl.when(has[d])
-        def _():
-            greet(toward[d])
-
-
-def await_greetings(has, others):
-    pl.semaphore_wait(
-        pltpu.get_barrier_semaphore(), others + has[1].astype(jnp.int32) + has[-1].astype(jnp.int32)
-    )
-
-
-def query_kernel(
-    n, groups, x_ref, gain_ref, wq_ref, wo_ref, q_ref, plane_ref,
-    xs, w2, local, zs, zr, cs, cr, ys, yr, gs, gr, ps, pr,
+def query_phase(
+    n, groups, x_ref, gain_ref, wq_ref, wo_ref, q_ref, w4, xs, w2, local, zs, zr, cs, cr, ys, yr, gs, gr, ps, pr
 ):
     A = n // 4
     me, a, b, c = place(n)
@@ -79,21 +60,22 @@
     rows = x_ref.shape[0]
     share = DH // groups
     twins = [lax.rem(mine + i, groups) for i in range(1, groups)]
-    greet_along(has, toward)
-    greet(across)
-    greet(pair)
+    for other in range(1, n):
+        greet(lax.rem(me + other, n))
     for twin in twins:
         pl.semaphore_signal(
             pltpu.get_barrier_semaphore(), inc=1, device_id={"groups": twin, "mp": me}, device_id_type=MESH
         )
     load_w = pltpu.make_async_copy(wq_ref, w2.at[b], local.at[0])
     load_w.start()
+    load_own = pltpu.make_async_copy(wo_ref, w4.at[0], local.at[1])
+    load_own.start()
     values = x_ref[...].astype(jnp.float32)
     scale = lax.rsqrt(jnp.mean(values * values, axis=-1, keepdims=True) + epsilon)
     for p in range(P):
         part = slice(p * W, (p + 1) * W)
         xs[p, a, c] = (values[:, part] * scale * gain_ref[:, part]).astype(jnp.bfloat16)
-    await_greetings(has, 1 + groups)
+    pl.semaphore_wait(pltpu.get_barrier_semaphore(), n + groups - 2)
 
     def z_copy(k, p, s, d):
         row = 0 if d == 1 else A
@@ -106,7 +88,7 @@
         return pl.ds(pl.multiple_of(part * share, share), share)
 
     def landing(which, bb, part):
-        return w2.at[bb, strip(part)] if which == 0 else plane_ref.at[1, strip(part)]
+        return w2.at[bb, strip(part)] if which == 0 else w4.at[2, strip(part)]
 
     def y_copy(which):
         source = (wq_ref, wo_ref)[which].at[strip(mine)]
@@ -123,8 +105,8 @@
             device_id={"groups": to, "mp": me}, device_id_type=MESH,
         )
 
-    plane_pair = remote(wo_ref, plane_ref.at[0], ps.at[0], pr.at[0], pair)
-    plane_diagonal = remote(plane_ref.at[1], plane_ref.at[2], ps.at[1], pr.at[1], pair)
+    plane_pair = remote(wo_ref, w4.at[1], ps.at[0], pr.at[0], pair)
+    plane_diagonal = remote(w4.at[2], w4.at[3], ps.at[1], pr.at[1], pair)
     for p in range(P):
         for d in (1, -1):
 
@@ -156,10 +138,8 @@
             y_arrival(s - 1).wait_recv()
             for twin in twins:
                 g_copy(s - 1, mine, twin).start()
-    for which in range(2):
-        for twin in twins:
-            g_copy(which, twin, mine).wait_recv()
-    plane_diagonal.start()
+    for twin in twins:
+        g_copy(0, twin, mine).wait_recv()
     load_w.wait()
     total = jnp.zeros((2 * A * rows, PAD), jnp.float32)
     for p in range(P):
@@ -170,163 +150,44 @@
             (((1,), (1,)), ((), ())), preferred_element_type=jnp.float32,
         )
     q_ref[...] = total.astype(jnp.bfloat16).reshape(2 * A, rows, PAD)
-    for s in range(A):
-        for d in (1, -1):
-            k = a - s * d
-
-            @pl.when((k >= 0) & (k < A) & has[d])
-            def _():
-                for p in range(P):
-                    z_copy(k, p, s, d).wait_send()
-
-    for k in range(A):
-        for p in range(P):
-            c_copy(k, p, c).wait_send()
-    for which in range(2):
-        y_copy(which).wait_send()
+
+    def share_diagonal():
         for twin in twins:
-            g_copy(which, mine, twin).wait_send()
-    plane_pair.wait()
-    plane_diagonal.wait()
-
-
-def make_query(hidden, gain, w_query, w_out, n, groups, number):
-    A = n // 4
-    assert A > 2 and DH % groups == 0
-    rows, width = hidden.shape
-    P = pieces_of(n, width)
-    W = width // P
-    half = jnp.bfloat16
-    return pl.pallas_call(
-        functools.partial(query_kernel, n, groups),
-        out_shape=[
-            jax.ShapeDtypeStruct((2 * A, rows, PAD), half),
-            jax.ShapeDtypeStruct((3,) + w_out.shape, half),
-        ],
-        in_specs=[pl.BlockSpec(memory_space=m) for m in (VM, VM, pl.ANY, pl.ANY)],
-        out_specs=[pl.BlockSpec(memory_space=VM), pl.BlockSpec(memory_space=pl.ANY)],
-        scratch_shapes=[
-            VM((P, A, 2, rows, W), half),
-            VM((2, DH, width), half),
-            DMA((1,)), DMA((2 * A, P)), DMA((A, P)), DMA((A, P)), DMA((A, P)),
-            DMA((2,)), DMA((2,)), DMA((2, groups)), DMA((2, groups)), DMA((2,)), DMA((2,)),
-        ],
-        compiler_params=params(number),
-        name=f"query_{number}",
-    )(hidden, gain[None, :], w_query.T, w_out)
-
-
-def project_kernel(
-    n, context_ref, hidden_ref, wo_ref, plane_ref, out_ref,
-    w4, c_send, c_recv, part, zsend, zright, zleft, local, cs, cr, zs, zr,
-):
-    A = n // 4
-    me, a, b, c = place(n)
-    peers = (index_of(a, b, 1 - c), index_of(a, 1 - b, c), index_of(a, 1 - b, 1 - c))
-    has, toward = neighbours(n)
-    landing = {1: zright, -1: zleft}
-    P, _, rows, W = part.shape
-    depth = wo_ref.shape[0]
-    greet_along(has, toward)
-    for peer in peers:
-        greet(peer)
-    load_own = pltpu.make_async_copy(wo_ref, w4.at[0], local.at[0])
-    load_plane = pltpu.make_async_copy(plane_ref, w4.at[pl.ds(1, 3)], local.at[1])
-    load_own.start()
-    load_plane.start()
-    for i, (bb, cc) in enumerate(((b, 1 - c), (1 - b, c), (1 - b, 1 - c))):
+            g_copy(1, twin, mine).wait_recv()
+        plane_diagonal.start()
+
+    def share_arrived():
+        load_own.wait()
+        plane_pair.wait_recv()
+        plane_diagonal.wait_recv()
+
+    def finish():
+        for s in range(A):
+            for d in (1, -1):
+                k = a - s * d
+
+                @pl.when((k >= 0) & (k < A) & has[d])
+                def _():
+                    for p in range(P):
+                        z_copy(k, p, s, d).wait_send()
+
         for k in range(A):
-            c_send[i, k] = context_ref[index_of(k, bb, cc)]
-    for k in range(A):
-        c_recv[0, k] = context_ref[index_of(k, b, c)]
-    await_greetings(has, 3)
-    swaps = [remote(c_send.at[i], c_recv.at[i + 1], cs.at[i], cr.at[i], peers[i]) for i in range(3)]
-    for i in (2, 1, 0):
-        swaps[i].start()
-    load_own.wait()
-    load_plane.wait()
-    for swap in swaps:
-        swap.wait_recv()
-    low = lax.broadcasted_iota(jnp.int32, (A * rows, PAD), 1) < DH
-
-    def beside(i):
-        first = c_recv[i].reshape(A * rows, PAD).astype(jnp.float32)
-        second = c_recv[i + 1].reshape(A * rows, PAD).astype(jnp.float32)
-        return jnp.where(low, pltpu.roll(first, DH, 1), second).astype(jnp.bfloat16)
-
-    left = jnp.concatenate([beside(0), beside(2)], axis=1)
-
-    def z_copy(k, p, d):
-        return remote(zsend.at[p, k], landing[d].at[p, k], zs.at[k, p], zr.at[(0 if d == 1 else A) + k, p], toward[d])
-
-    def z_arrival(k, p, d):
-        return remote(zsend.at[p, k], landing[d].at[p, k], zs.at[k, p], zr.at[(0 if d == 1 else A) + k, p], toward[-d])
-
-    for s in range(A - 1, -1, -1):
-        for p in range(P):
-            if s == A - 1:
-                w = w4[:, :, p * W : (p + 1) * W].reshape(4 * depth, W)
-                found = jnp.dot(left, w, preferred_element_type=jnp.float32)
-                part[p] = found.reshape(A, rows, W)
-            for d in (1, -1) if s else (1,):
-                k = a + s * d
-
-                @pl.when((k >= 0) & (k < A))
-                def _():
-                    for came in (d,) if s else (1, -1):
-
-                        @pl.when(has[-came])
-                        def _():
-                            z_arrival(k, p, came).wait_recv()
-                            part[p, k] = part[p, k] + landing[came][p, k].astype(jnp.float32)
-
-                    if s:
-                        zsend[p, k] = part[p, k].astype(jnp.bfloat16)
-                        z_copy(k, p, d).start()
-                    else:
-                        at = slice(p * W, (p + 1) * W)
-                        out_ref[:, at] = (hidden_ref[:, at].astype(jnp.float32) + part[p, k]).astype(jnp.bfloat16)
-
-    for s in range(A - 1, 0, -1):
-        for d in (1, -1):
-            k = a + s * d
-
-            @pl.when((k >= 0) & (k < A))
-            def _():
-                for p in range(P):
-                    z_copy(k, p, d).wait_send()
-
-    for swap in swaps:
-        swap.wait_send()
-
-
-def project(context, hidden, w_out, plane, n, number):
-    A = n // 4
-    rows, width = hidden.shape
-    P = pieces_of(n, width)
-    W = width // P
-    half = jnp.bfloat16
-    return pl.pallas_call(
-        functools.partial(project_kernel, n),
-        out_shape=jax.ShapeDtypeStruct((rows, width), half),
-        in_specs=[pl.BlockSpec(memory_space=m) for m in (VM, VM, pl.ANY, pl.ANY)],
-        out_specs=pl.BlockSpec(memory_space=VM),
-        scratch_shapes=[
-            VM((4,) + w_out.shape, half),
-            VM((3, A, rows, PAD), half),
-            VM((4, A, rows, PAD), half),
-            VM((P, A, rows, W), jnp.float32),
-        ]
-        + [VM((P, A, rows, W), half)] * 3
-        + [DMA((2,)), DMA((3,)), DMA((3,)), DMA((A, P)), DMA((2 * A, P))],
-        compiler_params=params(number),
-        name=f"project_{number}",
-    )(context, hidden, w_out, plane)
-
-
-def attend_kernel(
-    n, lengths_ref, q_ref, kv_ref, cached_ref, out_ref,
-    q_all, q_cached, kv, cached, scores, chances, o_send, o_recv, stats, st_send, st_recv,
+            for p in range(P):
+                c_copy(k, p, c).wait_send()
+        for which in range(2):
+            y_copy(which).wait_send()
+            for twin in twins:
+                g_copy(which, mine, twin).wait_send()
+        plane_pair.wait_send()
+        plane_diagonal.wait_send()
+
+    return share_diagonal, share_arrived, finish
+
+
+def attend_phase(
+    n, between, lengths_ref, q_ref, kv_ref, cached_ref, context_ref,
+    kv, cached, scores, chances, stats,
+    q_all, q_cached, o_send, o_recv, st_send, st_recv,
     local, qzs, qzr, qys, qyr, qcs, qcr, os, orr, ss, sr,
 ):
     A = n // 4
@@ -342,14 +203,11 @@
     load_kv.start()
     order = sorted(range(1, n), key=lambda s: -min(s, n - s))
     others = [lax.rem(me + s, n) for s in order]
-    for other in others:
-        greet(other)
     columns = [lax.rem(a + s, A) for s in range(1, A)]
     entering, flying = pl.ds(0, A), pl.ds(A, A)
     q_all[a, c, b] = q_ref[:A]
     q_cached[b] = q_ref[A:]
     stats[...] = jnp.zeros_like(stats)
-    pl.semaphore_wait(pltpu.get_barrier_semaphore(), n - 1)
 
     def qz_copy(to, k):
         return remote(q_ref.at[entering], q_all.at[k, c, b], qzs.at[to], qzr.at[k], index_of(to, b, c))
@@ -390,8 +248,12 @@
             parts.append(block((spot // 2) % 2, (spot // 4) * 2 + spot % 2))
         return parts[0] if per == 1 else jnp.concatenate(parts, axis=0)
 
+    def put(r, value):
+        per = QLEN // rows
+        for i in range(per):
+            context_ref[r * per + i] = value[i * rows : (i + 1) * rows].astype(jnp.bfloat16)
+
     def cached_request(r):
-        to = pl.ds(pl.multiple_of((requests + r) * QLEN, QLEN), QLEN)
         block = cached[r]
         query = request_of(r, lambda bb, spot: q_cached[bb, spot]).astype(jnp.float32)
         query = jnp.where(b == 0, query, pltpu.roll(query, DH, 1))
@@ -404,7 +266,7 @@
         exponent = jnp.exp(masked - jnp.max(masked, axis=-1, keepdims=True))
         inverse = 1.0 / jnp.sum(exponent, axis=-1, keepdims=True)
         weights = (exponent * inverse).astype(jnp.bfloat16)
-        out_ref[to, :] = jnp.dot(weights, block, preferred_element_type=jnp.float32).astype(jnp.bfloat16)
+        put(requests + r, jnp.dot(weights, block, preferred_element_type=jnp.float32))
 
     def cached_requests(start, stop):
         def two(i, carry):
@@ -416,24 +278,6 @@
         if (stop - start) % 2:
             cached_request(stop - 1)
 
-    for k in columns:
-        qz_copy(k, k).wait_recv()
-        qy_copy(k, b).start()
-        qc_copy(k, b, c).start()
-    cached_copy(1 - b).wait_recv()
-    load_cached.wait()
-    first, second = requests // 4, requests // 2
-    cached_requests(0, first)
-    qy_copy(a, 1 - b).wait_recv()
-    qc_copy(a, 1 - b, c).start()
-    for k in columns:
-        qy_copy(k, 1 - b).wait_recv()
-        qc_copy(k, 1 - b, c).start()
-    cached_requests(first, second)
-    load_kv.wait()
-    for k in range(A):
-        for bb in range(2):
-            qc_copy(k, bb, 1 - c).wait_recv()
     at_position = me * positions + lax.broadcasted_iota(jnp.int32, (1, positions), 1)
 
     def pair_step(step, carry):
@@ -486,7 +330,46 @@
             o_copy(other, me, step).start()
         return carry
 
-    lax.fori_loop(0, pairs, pair_step, 0)
+    def steps(column):
+        def one(i, carry):
+            return pair_step(2 * i + column, carry)
+
+        lax.fori_loop(0, pairs // 2, one, 0)
+
+    def second_column():
+        qy_copy(a, 1 - b).wait_recv()
+        qc_copy(a, 1 - b, c).start()
+        for k in columns:
+            qy_copy(k, 1 - b).wait_recv()
+            qc_copy(k, 1 - b, c).start()
+
+    def arrived(bb):
+        for k in range(A):
+            qc_copy(k, bb, 1 - c).wait_recv()
+
+    for k in columns:
+        qz_copy(k, k).wait_recv()
+        qy_copy(k, b).start()
+        qc_copy(k, b, c).start()
+    between()
+    cached_copy(1 - b).wait_recv()
+    load_cached.wait()
+    first, second = requests // 4, requests // 2
+    cached_requests(0, first)
+    load_kv.wait()
+    if rows == QLEN:
+        arrived(b)
+        steps(b)
+        second_column()
+    else:
+        second_column()
+        arrived(b)
+        arrived(1 - b)
+        steps(b)
+    cached_requests(first, second)
+    if rows == QLEN:
+        arrived(1 - b)
+    steps(1 - b)
     parts = QLEN // 8
     gap = PAD // parts
     folded = stats[:, :8, :].reshape(heads * 8, PAD)
@@ -519,51 +402,100 @@
                 share.append(jnp.where(short, known[:, lone + 1 : lone + 2], known[:, lone : lone + 1]))
             share = jnp.concatenate(share, axis=0)
             mixed = mixed + share * o_recv[d, step * QLEN : (step + 1) * QLEN, :].astype(jnp.float32)
-        out_ref[2 * step * QLEN : (2 * step + 1) * QLEN, :] = mixed.astype(jnp.bfloat16)
-        out_ref[(2 * step + 1) * QLEN : (2 * step + 2) * QLEN, :] = pltpu.roll(mixed, DH, 1).astype(jnp.bfloat16)
-    for k in columns:
-        qz_copy(k, a).wait_send()
-    cached_copy(b).wait_send()
+        put(2 * step, mixed)
+        put(2 * step + 1, pltpu.roll(mixed, DH, 1))
+
+    def finish():
+        for k in columns:
+            qz_copy(k, a).wait_send()
+        cached_copy(b).wait_send()
+        for k in range(A):
+            qy_copy(k, b).wait_send()
+            for bb in range(2):
+                qc_copy(k, bb, c).wait_send()
+        for other in others:
+            st_copy(other, me).wait_send()
+            for step in range(pairs):
+                o_copy(other, me, step).wait_send()
+
+    return finish
+
+
+def project_phase(
+    n, arrived, context_ref, hidden_ref, out_ref, w4, part, c_send, c_recv, zsend, zright, zleft, cs, cr, zs, zr
+):
+    A = n // 4
+    me, a, b, c = place(n)
+    peers = (index_of(a, b, 1 - c), index_of(a, 1 - b, c), index_of(a, 1 - b, 1 - c))
+    has, toward = neighbours(n)
+    landing = {1: zright, -1: zleft}
+    P, _, rows, W = part.shape
+    depth = w4.shape[1]
+    for i, (bb, cc) in enumerate(((b, 1 - c), (1 - b, c), (1 - b, 1 - c))):
+        for k in range(A):
+            c_send[i, k] = context_ref[index_of(k, bb, cc)]
     for k in range(A):
-        qy_copy(k, b).wait_send()
-        for bb in range(2):
-            qc_copy(k, bb, c).wait_send()
-    for other in others:
-        st_copy(other, me).wait_send()
-        for step in range(pairs):
-            o_copy(other, me, step).wait_send()
-
-
-def attend(query, entering_kv, cached_kv, lengths, n, number):
-    A = n // 4
-    requests, positions, width = entering_kv.shape
-    pairs, heads = requests // 2, width // PAD
-    rows = query.shape[1]
-    assert heads == n and QLEN % rows == 0 and 8 * requests <= PAD
-    half, full = jnp.bfloat16, jnp.float32
-    return pl.pallas_call(
-        functools.partial(attend_kernel, n),
-        out_shape=jax.ShapeDtypeStruct((2 * requests * QLEN, PAD), half),
-        in_specs=[pl.BlockSpec(memory_space=m) for m in (pltpu.SMEM, VM, pl.ANY, pl.ANY)],
-        out_specs=pl.BlockSpec(memory_space=VM),
-        scratch_shapes=[
-            VM((A, 2, 2, A, rows, PAD), half),
-            VM((2, A, rows, PAD), half),
-            VM(entering_kv.shape, half),
-            VM(cached_kv.shape, half),
-            VM((2, heads // 2, 2 * QLEN, positions), full),
-            VM((2, heads // 2, 2 * QLEN, positions), half),
-            VM((n, pairs * QLEN, PAD), half),
-            VM((n, pairs * QLEN, PAD), half),
-            VM((n, QLEN, PAD), full),
-            VM((n, 8, PAD), full),
-            VM((n, 8, PAD), full),
-            DMA((2,)), DMA((A,)), DMA((A,)), DMA((A + 1,)), DMA((A + 1,)), DMA((2 * A,)), DMA((2 * A,)),
-            DMA((pairs, n)), DMA((pairs, n)), DMA((n,)), DMA((n,)),
-        ],
-        compiler_params=params(number),
-        name=f"attend_{number}",
-    )(lengths, query, entering_kv, cached_kv)
+        c_recv[0, k] = context_ref[index_of(k, b, c)]
+    swaps = [remote(c_send.at[i], c_recv.at[i + 1], cs.at[i], cr.at[i], peers[i]) for i in range(3)]
+    for i in (2, 1, 0):
+        swaps[i].start()
+    arrived()
+    for swap in swaps:
+        swap.wait_recv()
+    low = lax.broadcasted_iota(jnp.int32, (A * rows, PAD), 1) < DH
+
+    def beside(i):
+        first = c_recv[i].reshape(A * rows, PAD).astype(jnp.float32)
+        second = c_recv[i + 1].reshape(A * rows, PAD).astype(jnp.float32)
+        return jnp.where(low, pltpu.roll(first, DH, 1), second).astype(jnp.bfloat16)
+
+    left = jnp.concatenate([beside(0), beside(2)], axis=1)
+
+    def z_copy(k, p, d):
+        return remote(zsend.at[p, k], landing[d].at[p, k], zs.at[k, p], zr.at[(0 if d == 1 else A) + k, p], toward[d])
+
+    def z_arrival(k, p, d):
+        return remote(zsend.at[p, k], landing[d].at[p, k], zs.at[k, p], zr.at[(0 if d == 1 else A) + k, p], toward[-d])
+
+    for s in range(A - 1, -1, -1):
+        for p in range(P):
+            if s == A - 1:
+                w = w4[:, :, p * W : (p + 1) * W].reshape(4 * depth, W)
+                found = jnp.dot(left, w, preferred_element_type=jnp.float32)
+                part[p] = found.reshape(A, rows, W)
+            for d in (1, -1) if s else (1,):
+                k = a + s * d
+
+                @pl.when((k >= 0) & (k < A))
+                def _():
+                    for came in (d,) if s else (1, -1):
+
+                        @pl.when(has[-came])
+                        def _():
+                            z_arrival(k, p, came).wait_recv()
+                            part[p, k] = part[p, k] + landing[came][p, k].astype(jnp.float32)
+
+                    if s:
+                        zsend[p, k] = part[p, k].astype(jnp.bfloat16)
+                        z_copy(k, p, d).start()
+                    else:
+                        at = slice(p * W, (p + 1) * W)
+                        out_ref[:, at] = (hidden_ref[:, at].astype(jnp.float32) + part[p, k]).astype(jnp.bfloat16)
+
+    def finish():
+        for s in range(A - 1, 0, -1):
+            for d in (1, -1):
+                k = a + s * d
+
+                @pl.when((k >= 0) & (k < A))
+                def _():
+                    for p in range(P):
+                        z_copy(k, p, d).wait_send()
+
+        for swap in swaps:
+            swap.wait_send()
+
+    return finish
 
 
 def far_first(A, a):
@@ -576,9 +508,10 @@
     return found
 
 
-def feed_kernel(
+def feed_phase(
     n, x_ref, gain_ref, gate_ref, up_ref, down_ref, out_ref,
-    xs, w_gate, w_up, w_down, gates, ups, act, part, cbuf, ysend, yrecv, zsend, zland,
+    w_in, sums_in, w_down, act, part,
+    xs, cbuf, ysend, yrecv, zsend, zland,
     local, zs, zr, ys, yr, cs, cr, gs, gr, hs, hr, ts, tr,
 ):
     A = n // 4
@@ -587,12 +520,12 @@
     has, toward = neighbours(n)
     P, W = xs.shape[0], xs.shape[-1]
     rows = x_ref.shape[0]
-    greet_along(has, toward)
-    greet(across)
-    greet(pair)
+    units = gate_ref.shape[1]
+    split = [(w_in[0], slice(0, units)), (w_in[-1], slice(units, 2 * units) if len(w_in) == 1 else slice(0, units))]
     loads = [
-        pltpu.make_async_copy(src, dst, local.at[i])
-        for i, (src, dst) in enumerate(((gate_ref, w_gate), (up_ref, w_up), (down_ref, w_down)))
+        pltpu.make_async_copy(gate_ref, split[0][0].at[:, split[0][1]], local.at[0]),
+        pltpu.make_async_copy(up_ref, split[1][0].at[:, split[1][1]], local.at[1]),
+        pltpu.make_async_copy(down_ref, w_down, local.at[2]),
     ]
     for load in loads:
         load.start()
@@ -601,7 +534,6 @@
     for p in range(P):
         at = slice(p * W, (p + 1) * W)
         xs[p, b, c, a] = (values[:, at] * scale * gain_ref[:, at]).astype(jnp.bfloat16)
-    await_greetings(has, 2)
 
     def z_copy(k, p, s, d):
         block = xs.at[p, b, c, k]
@@ -664,7 +596,7 @@
             for k in range(A):
                 c_copy(k, p, bb, 1 - c).wait_recv()
         left = xs[p].reshape(n * rows, W)
-        for w, sums in ((w_gate, gates), (w_up, ups)):
+        for w, sums in zip(w_in, sums_in):
             found = jnp.dot(left, w[p * W : (p + 1) * W, :], preferred_element_type=jnp.float32)
             sums[...] = found if p == 0 else sums[...] + found
 
@@ -690,7 +622,8 @@
     tall = A * rows
     for group in range(4):
         at = slice(group * tall, (group + 1) * tall)
-        act[group] = (jax.nn.gelu(gates[at, :], approximate=True) * ups[at, :]).astype(jnp.bfloat16)
+        gate, up = sums_in[0][at, split[0][1]], sums_in[-1][at, split[1][1]]
+        act[group] = (jax.nn.gelu(gate, approximate=True) * up).astype(jnp.bfloat16)
 
     def multiply(i, p, bb, cc):
         found = jnp.dot(act[2 * bb + cc], w_down[:, p * W : (p + 1) * W], preferred_element_type=jnp.float32)
@@ -773,60 +706,110 @@
         g_copy(1, p).wait_send()
 
 
-def feed(residual, gain, w_gate, w_up, w_down, n, number):
+def layer_kernel(n, groups, counts, *refs):
+    ends = [sum(counts[: i + 1]) for i in range(len(counts))]
+    inputs, (out_ref,), shared, ask, look, out, give = (
+        refs[end - count : end] for end, count in zip(ends, counts)
+    )
+    hidden_ref, gain_ref, wq_ref, kv_ref, cached_ref, lengths_ref, wo_ref, ffn_gain, gate_ref, up_ref, down_ref = inputs
+    q_ref, w4, context_ref, residual = shared
+    half, full = jnp.bfloat16, jnp.float32
+    rows, width = hidden_ref.shape
+    requests, positions, across = kv_ref.shape
+    heads, units = across // PAD, gate_ref.shape[1]
+    P = pieces_of(n, width)
+    A, W = n // 4, width // P
+    diagonal, arrived, end_query = query_phase(
+        n, groups, hidden_ref, gain_ref, wq_ref, wo_ref, q_ref, w4, *ask
+    )
+
+    def attending(*own):
+        attend_phase(n, diagonal, lengths_ref, q_ref, kv_ref, cached_ref, context_ref, *own, *look)()
+
+    pl.run_scoped(
+        attending,
+        VM(kv_ref.shape, half),
+        VM(cached_ref.shape, half),
+        VM((2, heads // 2, 2 * QLEN, positions), full),
+        VM((2, heads // 2, 2 * QLEN, positions), half),
+        VM((n, QLEN, PAD), full),
+    )
+
+    def projecting(part):
+        project_phase(n, arrived, context_ref, hidden_ref, residual, w4, part, *out)()
+
+    pl.run_scoped(projecting, VM((P, A, rows, W), full))
+    joined = 1 if units % PAD == 0 else 2
+    wide = 2 * units // joined
+
+    def feeding(*own):
+        feed_phase(
+            n, residual, ffn_gain, gate_ref, up_ref, down_ref, out_ref,
+            own[:joined], own[joined : 2 * joined], *own[2 * joined :], *give,
+        )
+
+    pl.run_scoped(
+        feeding,
+        *[VM((width, wide), half)] * joined,
+        *[VM((n * rows, wide), full)] * joined,
+        VM(down_ref.shape, half),
+        VM((4, A * rows, units), half),
+        VM((4, P, A, rows, W), full),
+    )
+    end_query()
+
+
+def layer(n, groups, hidden, gain, w_query, entering_kv, cached_kv, lengths, w_out, ffn_gain, w_gate, w_up, w_down):
     A = n // 4
-    rows, width = residual.shape
-    hidden_units = w_gate.shape[1]
+    rows, width = hidden.shape
+    requests, positions, across = entering_kv.shape
+    pairs, heads = requests // 2, across // PAD
+    assert A > 2 and DH % groups == 0 and pairs % 2 == 0
+    assert heads == n and QLEN % rows == 0 and 8 * requests <= PAD
     P = pieces_of(n, width)
     W = width // P
     half, full = jnp.bfloat16, jnp.float32
+    piece = (P, A, rows, W)
+    inputs = (
+        hidden, gain[None, :], w_query.T, entering_kv, cached_kv, lengths, w_out, ffn_gain[None, :],
+        w_gate, w_up, w_down,
+    )
+    spaces = (VM, VM, pl.ANY, pl.ANY, pl.ANY, pltpu.SMEM, pl.ANY, VM, pl.ANY, pl.ANY, pl.ANY)
+    shared = [
+        VM((2 * A, rows, PAD), half), VM((4,) + w_out.shape, half), VM((n, rows, PAD), half), VM((rows, width), half),
+    ]
+    ask = [
+        VM((P, A, 2, rows, W), half), VM((2, DH, width), half),
+        DMA((2,)), DMA((2 * A, P)), DMA((A, P)), DMA((A, P)), DMA((A, P)),
+        DMA((2,)), DMA((2,)), DMA((2, groups)), DMA((2, groups)), DMA((2,)), DMA((2,)),
+    ]
+    look = [
+        VM((A, 2, 2, A, rows, PAD), half), VM((2, A, rows, PAD), half),
+        VM((n, pairs * QLEN, PAD), half), VM((n, pairs * QLEN, PAD), half),
+        VM((n, 8, PAD), full), VM((n, 8, PAD), full),
+        DMA((2,)), DMA((A,)), DMA((A,)), DMA((A + 1,)), DMA((A + 1,)), DMA((2 * A,)), DMA((2 * A,)),
+        DMA((pairs, n)), DMA((pairs, n)), DMA((n,)), DMA((n,)),
+    ]
+    out = [VM((3, A, rows, PAD), half), VM((4, A, rows, PAD), half), VM(piece, half), VM(piece, half), VM(piece, half)]
+    out += [DMA((3,)), DMA((3,)), DMA((A, P)), DMA((2 * A, P))]
+    give = [
+        VM((P, 2, 2, A, rows, W), half), VM((2,) + piece, full),
+        VM(piece, half), VM(piece, half), VM(piece, half), VM((2,) + piece, half),
+        DMA((3,)), DMA((2 * A, P)), DMA((A, P)), DMA((A, P)), DMA((A, P)), DMA((2 * A, P)), DMA((2 * A, P)),
+        DMA((2, P)), DMA((2, P)), DMA((A, P)), DMA((A, P)), DMA((A, P)), DMA((2, A, P)),
+    ]
+    parts = (inputs, (None,), shared, ask, look, out, give)
     return pl.pallas_call(
-        functools.partial(feed_kernel, n),
+        functools.partial(layer_kernel, n, groups, tuple(len(part) for part in parts)),
         out_shape=jax.ShapeDtypeStruct((rows, width), half),
-        in_specs=[pl.BlockSpec(memory_space=m) for m in (VM, VM, pl.ANY, pl.ANY, pl.ANY)],
+        in_specs=[pl.BlockSpec(memory_space=m) for m in spaces],
         out_specs=pl.BlockSpec(memory_space=VM),
-        scratch_shapes=[
-            VM((P, 2, 2, A, rows, W), half),
-            VM(w_gate.shape, half),
-            VM(w_up.shape, half),
-            VM(w_down.shape, half),
-            VM((n * rows, hidden_units), full),
-            VM((n * rows, hidden_units), full),
-            VM((4, A * rows, hidden_units), half),
-            VM((4, P, A, rows, W), full),
-            VM((2, P, A, rows, W), full),
-        ]
-        + [VM((P, A, rows, W), half)] * 3
-        + [VM((2, P, A, rows, W), half)]
-        + [
-            DMA((3,)), DMA((2 * A, P)), DMA((A, P)), DMA((A, P)), DMA((A, P)), DMA((2 * A, P)), DMA((2 * A, P)),
-            DMA((2, P)), DMA((2, P)), DMA((A, P)), DMA((A, P)), DMA((A, P)), DMA((2, A, P)),
-        ],
-        compiler_params=params(number),
-        name=f"feed_{number}",
-    )(residual, gain[None, :], w_gate, w_up, w_down)
-
-
-def per_device(
-    n,
-    groups,
-    hidden,
-    norm_gain_attn,
-    w_query,
-    entering_kv,
-    cached_kv,
-    enc_lengths,
-    w_out,
-    norm_gain_ffn,
-    w_gate,
-    w_up,
-    w_down,
-):
-    rows, width = hidden.shape
-    query, plane = make_query(hidden, norm_gain_attn, w_query, w_out, n, groups, 0)
-    context = attend(query, entering_kv, cached_kv, enc_lengths, n, 1)
-    residual = project(context.reshape(n, rows, PAD), hidden, w_out, plane, n, 3)
-    return feed(residual, norm_gain_ffn, w_gate, w_up, w_down, n, 4)
+        scratch_shapes=shared + ask + look + out + give,
+        compiler_params=pltpu.CompilerParams(
+            collective_id=0, has_side_effects=True, vmem_limit_bytes=60 * 2**20
+        ),
+        name="layer",
+    )(*inputs)
 
 
 def solution(mesh):
@@ -844,7 +827,7 @@
         P("mp", None),
     )
     return jax.shard_map(
-        functools.partial(per_device, mesh.shape["mp"], mesh.shape["groups"]),
+        functools.partial(layer, mesh.shape["mp"], mesh.shape["groups"]),
         mesh=mesh,
         in_specs=placed,
         out_specs=P(("groups", "mp"), None),

time: 152 us -> 139 us (0.914)
  Pallas kernels: 150 us -> 137 us
    pallas_call x4 -> x1, Pallas kernels: 150 us -> 137 us  [layer(): pl.pallas_call(functools.partial(layer_kernel, n, groups, tuple((len(part...]
where the time goes in v4:
time: 139 us; the launch traced here: 138 us
  Pallas kernels  137 us (99%)
  local copies, waits for them, and re-layouts  1.67 us (1%)
    pallas_call x1, Pallas kernels, layer(): pl.pallas_call(functools.partial(layer_kernel, n, groups, tuple((len(part...  137 us

profile of v4, /device:TPU:0, one launch (start us, length us, event | category | flops | bytes accessed | tf_op | source)
XLA Modules:
  0.0 138.4 jit_solution(942591109995344607)
XLA Ops:
  0.0 136.8 %layer.1 = bf16[32,4096]{1,0:T(8,128)(2,1)} custom-call(bf16[32,4096]{1,0:T(8,128)(2,1)} %refs_0_.1, f32[1,4096]{1,0:T(1,128)} %bitcast.4, bf16[64,4096]{1,0:T(8,128)(2,1)} %bitcast.3, bf16[8,128,2048]{2,1,0:T(8,128)(2,1)} %refs_3_.1, bf16[8,2048,128]{2,1,0:T(8,128)(2,1)} %refs_4_.1, s32[2,8]{1,0:T(2,128)} %refs_5_.1, bf16[64,4096]{1,0:T(8,128)(2,1)} %refs_6_.1, ...), custom_call_target="tpu_custom_call" | custom-call | tf_op jit(solution)/shard_map/layer/pallas_call | solution.py:802
  136.8 1.7 %copy.13 = bf16[32,4096]{1,0:T(8,128)(2,1)} copy(bf16[32,4096]{1,0:T(8,128)(2,1)} %layer.1) | data formatting | bytes 524288

commit v5 on v4

--- a/solution.py
+++ b/solution.py
@@ -49,7 +49,7 @@
 
 
 def query_phase(
-    n, groups, x_ref, gain_ref, wq_ref, wo_ref, q_ref, w4, xs, w2, local, zs, zr, cs, cr, ys, yr, gs, gr, ps, pr
+    n, groups, x_ref, gain_ref, wq_ref, wo_ref, q_ref, w8, xs, w2, local, zs, zr, cs, cr, ys, yr, gs, gr, ps, pr, es, er
 ):
     A = n // 4
     me, a, b, c = place(n)
@@ -68,7 +68,7 @@
         )
     load_w = pltpu.make_async_copy(wq_ref, w2.at[b], local.at[0])
     load_w.start()
-    load_own = pltpu.make_async_copy(wo_ref, w4.at[0], local.at[1])
+    load_own = pltpu.make_async_copy(wo_ref, w8.at[0], local.at[1])
     load_own.start()
     values = x_ref[...].astype(jnp.float32)
     scale = lax.rsqrt(jnp.mean(values * values, axis=-1, keepdims=True) + epsilon)
@@ -88,7 +88,7 @@
         return pl.ds(pl.multiple_of(part * share, share), share)
 
     def landing(which, bb, part):
-        return w2.at[bb, strip(part)] if which == 0 else w4.at[2, strip(part)]
+        return w2.at[bb, strip(part)] if which == 0 else w8.at[2, strip(part)]
 
     def y_copy(which):
         source = (wq_ref, wo_ref)[which].at[strip(mine)]
@@ -105,8 +105,8 @@
             device_id={"groups": to, "mp": me}, device_id_type=MESH,
         )
 
-    plane_pair = remote(wo_ref, w4.at[1], ps.at[0], pr.at[0], pair)
-    plane_diagonal = remote(w4.at[2], w4.at[3], ps.at[1], pr.at[1], pair)
+    plane_pair = remote(wo_ref, w8.at[1], ps.at[0], pr.at[0], pair)
+    plane_diagonal = remote(w8.at[2], w8.at[3], ps.at[1], pr.at[1], pair)
     for p in range(P):
         for d in (1, -1):
 
@@ -151,15 +151,54 @@
         )
     q_ref[...] = total.astype(jnp.bfloat16).reshape(2 * A, rows, PAD)
 
-    def share_diagonal():
+    def own_strip(slot):
+        return w8.at[slot, strip(mine)]
+
+    beyond = remote(wo_ref.at[strip(mine)], own_strip(4), es.at[0], er.at[0], index_of(a + 1 - 2 * (a % 2), b, c))
+    beyond_across = remote(own_strip(4), own_strip(6), es.at[1], er.at[1], across)
+    beyond_pair = remote(w8.at[4], w8.at[5], es.at[2], er.at[2], pair)
+    beyond_diagonal = remote(w8.at[6], w8.at[7], es.at[3], er.at[3], pair)
+
+    def t_copy(i, part, to):
+        spot = w8.at[4 + 2 * i, strip(part)]
+        return pltpu.make_async_remote_copy(
+            src_ref=spot, dst_ref=spot, send_sem=gs.at[2 + i, to], recv_sem=gr.at[2 + i, part],
+            device_id={"groups": to, "mp": me}, device_id_type=MESH,
+        )
+
+    def share_first():
+        beyond.start()
+
+    def share_second():
         for twin in twins:
             g_copy(1, twin, mine).wait_recv()
         plane_diagonal.start()
+
+    def share_third():
+        beyond.wait_recv()
+        beyond_across.start()
+        for twin in twins:
+            t_copy(0, mine, twin).start()
+
+    def share_fourth():
+        beyond_across.wait_recv()
+        for twin in twins:
+            t_copy(1, mine, twin).start()
+        for twin in twins:
+            t_copy(0, twin, mine).wait_recv()
+        beyond_pair.start()
+
+    def share_fifth():
+        for twin in twins:
+            t_copy(1, twin, mine).wait_recv()
+        beyond_diagonal.start()
 
     def share_arrived():
         load_own.wait()
         plane_pair.wait_recv()
         plane_diagonal.wait_recv()
+        beyond_pair.wait_recv()
+        beyond_diagonal.wait_recv()
 
     def finish():
         for s in range(A):
@@ -180,8 +219,13 @@
                 g_copy(which, mine, twin).wait_send()
         plane_pair.wait_send()
         plane_diagonal.wait_send()
-
-    return share_diagonal, share_arrived, finish
+        for copy in (beyond, beyond_across, beyond_pair, beyond_diagonal):
+            copy.wait_send()
+        for i in range(2):
+            for twin in twins:
+                t_copy(i, mine, twin).wait_send()
+
+    return (share_first, share_second, share_third, share_fourth, share_fifth), share_arrived, finish
 
 
 def attend_phase(
@@ -237,6 +281,7 @@
     qy_copy(a, b, q_ref.at[entering]).start()
     cached_copy(b).start()
     qc_copy(a, b, c, q_ref.at[entering]).start()
+    between[0]()
     lane = lax.broadcasted_iota(jnp.int32, (QLEN, PAD), 1)
     low = lane < DH
 
@@ -351,7 +396,7 @@
         qz_copy(k, k).wait_recv()
         qy_copy(k, b).start()
         qc_copy(k, b, c).start()
-    between()
+    between[1]()
     cached_copy(1 - b).wait_recv()
     load_cached.wait()
     first, second = requests // 4, requests // 2
@@ -366,6 +411,7 @@
         arrived(b)
         arrived(1 - b)
         steps(b)
+    between[2]()
     cached_requests(first, second)
     if rows == QLEN:
         arrived(1 - b)
@@ -381,6 +427,7 @@
     o_recv[me] = o_send[me]
     st_recv[me] = st_send[me]
     cached_requests(second, requests)
+    between[3]()
     for other in others:
         st_copy(other, other).wait_recv()
     largest = st_recv[...]
@@ -422,51 +469,62 @@
 
 
 def project_phase(
-    n, arrived, context_ref, hidden_ref, out_ref, w4, part, c_send, c_recv, zsend, zright, zleft, cs, cr, zs, zr
+    n, start, arrived, context_ref, hidden_ref, out_ref, w8, part, c_send, c_recv, zsend, zright, zleft, cs, cr, zs, zr
 ):
-    A = n // 4
+    M = n // 8
     me, a, b, c = place(n)
-    peers = (index_of(a, b, 1 - c), index_of(a, 1 - b, c), index_of(a, 1 - b, 1 - c))
-    has, toward = neighbours(n)
+    m, e = a // 2, a % 2
+    has = {1: m < M - 1, -1: m > 0}
+    toward = {1: me + 8, -1: me - 8}
     landing = {1: zright, -1: zleft}
     P, _, rows, W = part.shape
-    depth = w4.shape[1]
-    for i, (bb, cc) in enumerate(((b, 1 - c), (1 - b, c), (1 - b, 1 - c))):
-        for k in range(A):
-            c_send[i, k] = context_ref[index_of(k, bb, cc)]
-    for k in range(A):
-        c_recv[0, k] = context_ref[index_of(k, b, c)]
-    swaps = [remote(c_send.at[i], c_recv.at[i + 1], cs.at[i], cr.at[i], peers[i]) for i in range(3)]
-    for i in (2, 1, 0):
-        swaps[i].start()
-    arrived()
+    depth = w8.shape[1]
+
+    def peer(j):
+        return e + (j // 4) * (1 - 2 * e), b + (j // 2 % 2) * (1 - 2 * b), c + (j % 2) * (1 - 2 * c)
+
+    swaps = []
+    for j in range(7, -1, -1):
+        ee, bb, cc = peer(j)
+        for k in range(M):
+            block = context_ref[index_of(2 * k + ee, bb, cc)]
+            if j:
+                c_send[j - 1, k] = block
+            else:
+                c_recv[0, k] = block
+        if j:
+            swap = remote(c_send.at[j - 1], c_recv.at[j], cs.at[j - 1], cr.at[j - 1], index_of(2 * m + ee, bb, cc))
+            swap.start()
+            swaps.append(swap)
+    start()
     for swap in swaps:
         swap.wait_recv()
-    low = lax.broadcasted_iota(jnp.int32, (A * rows, PAD), 1) < DH
+    low = lax.broadcasted_iota(jnp.int32, (M * rows, PAD), 1) < DH
 
     def beside(i):
-        first = c_recv[i].reshape(A * rows, PAD).astype(jnp.float32)
-        second = c_recv[i + 1].reshape(A * rows, PAD).astype(jnp.float32)
+        first = c_recv[i].reshape(M * rows, PAD).astype(jnp.float32)
+        second = c_recv[i + 1].reshape(M * rows, PAD).astype(jnp.float32)
         return jnp.where(low, pltpu.roll(first, DH, 1), second).astype(jnp.bfloat16)
 
-    left = jnp.concatenate([beside(0), beside(2)], axis=1)
+    left = jnp.concatenate([beside(i) for i in range(0, 8, 2)], axis=1)
+    arrived()
 
     def z_copy(k, p, d):
-        return remote(zsend.at[p, k], landing[d].at[p, k], zs.at[k, p], zr.at[(0 if d == 1 else A) + k, p], toward[d])
+        return remote(zsend.at[p, k], landing[d].at[p, k], zs.at[k, p], zr.at[(0 if d == 1 else M) + k, p], toward[d])
 
     def z_arrival(k, p, d):
-        return remote(zsend.at[p, k], landing[d].at[p, k], zs.at[k, p], zr.at[(0 if d == 1 else A) + k, p], toward[-d])
-
-    for s in range(A - 1, -1, -1):
+        return remote(zsend.at[p, k], landing[d].at[p, k], zs.at[k, p], zr.at[(0 if d == 1 else M) + k, p], toward[-d])
+
+    for s in range(M - 1, -1, -1):
         for p in range(P):
-            if s == A - 1:
-                w = w4[:, :, p * W : (p + 1) * W].reshape(4 * depth, W)
+            if s == M - 1:
+                w = w8[:, :, p * W : (p + 1) * W].reshape(8 * depth, W)
                 found = jnp.dot(left, w, preferred_element_type=jnp.float32)
-                part[p] = found.reshape(A, rows, W)
+                part[p] = found.reshape(M, rows, W)
             for d in (1, -1) if s else (1,):
-                k = a + s * d
-
-                @pl.when((k >= 0) & (k < A))
+                k = m + s * d
+
+                @pl.when((k >= 0) & (k < M))
                 def _():
                     for came in (d,) if s else (1, -1):
 
@@ -483,11 +541,11 @@
                         out_ref[:, at] = (hidden_ref[:, at].astype(jnp.float32) + part[p, k]).astype(jnp.bfloat16)
 
     def finish():
-        for s in range(A - 1, 0, -1):
+        for s in range(M - 1, 0, -1):
             for d in (1, -1):
-                k = a + s * d
-
-                @pl.when((k >= 0) & (k < A))
+                k = m + s * d
+
+                @pl.when((k >= 0) & (k < M))
                 def _():
                     for p in range(P):
                         z_copy(k, p, d).wait_send()
@@ -712,19 +770,19 @@
         refs[end - count : end] for end, count in zip(ends, counts)
     )
     hidden_ref, gain_ref, wq_ref, kv_ref, cached_ref, lengths_ref, wo_ref, ffn_gain, gate_ref, up_ref, down_ref = inputs
-    q_ref, w4, context_ref, residual = shared
+    q_ref, w8, context_ref, residual = shared
     half, full = jnp.bfloat16, jnp.float32
     rows, width = hidden_ref.shape
     requests, positions, across = kv_ref.shape
     heads, units = across // PAD, gate_ref.shape[1]
     P = pieces_of(n, width)
     A, W = n // 4, width // P
-    diagonal, arrived, end_query = query_phase(
-        n, groups, hidden_ref, gain_ref, wq_ref, wo_ref, q_ref, w4, *ask
+    shares, arrived, end_query = query_phase(
+        n, groups, hidden_ref, gain_ref, wq_ref, wo_ref, q_ref, w8, *ask
     )
 
     def attending(*own):
-        attend_phase(n, diagonal, lengths_ref, q_ref, kv_ref, cached_ref, context_ref, *own, *look)()
+        attend_phase(n, shares, lengths_ref, q_ref, kv_ref, cached_ref, context_ref, *own, *look)()
 
     pl.run_scoped(
         attending,
@@ -736,9 +794,9 @@
     )
 
     def projecting(part):
-        project_phase(n, arrived, context_ref, hidden_ref, residual, w4, part, *out)()
-
-    pl.run_scoped(projecting, VM((P, A, rows, W), full))
+        project_phase(n, shares[4], arrived, context_ref, hidden_ref, residual, w8, part, *out)()
+
+    pl.run_scoped(projecting, VM((P, A // 2, rows, W), full))
     joined = 1 if units % PAD == 0 else 2
     wide = 2 * units // joined
 
@@ -764,7 +822,7 @@
     rows, width = hidden.shape
     requests, positions, across = entering_kv.shape
     pairs, heads = requests // 2, across // PAD
-    assert A > 2 and DH % groups == 0 and pairs % 2 == 0
+    assert A > 2 and A % 2 == 0 and DH % groups == 0 and pairs % 2 == 0
     assert heads == n and QLEN % rows == 0 and 8 * requests <= PAD
     P = pieces_of(n, width)
     W = width // P
@@ -776,12 +834,12 @@
     )
     spaces = (VM, VM, pl.ANY, pl.ANY, pl.ANY, pltpu.SMEM, pl.ANY, VM, pl.ANY, pl.ANY, pl.ANY)
     shared = [
-        VM((2 * A, rows, PAD), half), VM((4,) + w_out.shape, half), VM((n, rows, PAD), half), VM((rows, width), half),
+        VM((2 * A, rows, PAD), half), VM((8,) + w_out.shape, half), VM((n, rows, PAD), half), VM((rows, width), half),
     ]
     ask = [
         VM((P, A, 2, rows, W), half), VM((2, DH, width), half),
         DMA((2,)), DMA((2 * A, P)), DMA((A, P)), DMA((A, P)), DMA((A, P)),
-        DMA((2,)), DMA((2,)), DMA((2, groups)), DMA((2, groups)), DMA((2,)), DMA((2,)),
+        DMA((2,)), DMA((2,)), DMA((4, groups)), DMA((4, groups)), DMA((2,)), DMA((2,)), DMA((4,)), DMA((4,)),
     ]
     look = [
         VM((A, 2, 2, A, rows, PAD), half), VM((2, A, rows, PAD), half),
@@ -790,8 +848,10 @@
         DMA((2,)), DMA((A,)), DMA((A,)), DMA((A + 1,)), DMA((A + 1,)), DMA((2 * A,)), DMA((2 * A,)),
         DMA((pairs, n)), DMA((pairs, n)), DMA((n,)), DMA((n,)),
     ]
-    out = [VM((3, A, rows, PAD), half), VM((4, A, rows, PAD), half), VM(piece, half), VM(piece, half), VM(piece, half)]
-    out += [DMA((3,)), DMA((3,)), DMA((A, P)), DMA((2 * A, P))]
+    M = A // 2
+    half_piece = (P, M, rows, W)
+    out = [VM((7, M, rows, PAD), half), VM((8, M, rows, PAD), half)] + [VM(half_piece, half)] * 3
+    out += [DMA((7,)), DMA((7,)), DMA((M, P)), DMA((2 * M, P))]
     give = [
         VM((P, 2, 2, A, rows, W), half), VM((2,) + piece, full),
         VM(piece, half), VM(piece, half), VM(piece, half), VM((2,) + piece, half),

time: 139 us -> 137 us (0.986)
  Pallas kernels: 137 us -> 135 us
    pallas_call x1, Pallas kernels: 137 us -> 135 us  [layer(): pl.pallas_call(functools.partial(layer_kernel, n, groups, tuple((len(part...]
where the time goes in v5:
time: 137 us; the launch traced here: 136 us
  Pallas kernels  135 us (99%)
  local copies, waits for them, and re-layouts  1.67 us (1%)
    pallas_call x1, Pallas kernels, layer(): pl.pallas_call(functools.partial(layer_kernel, n, groups, tuple((len(part...  135 us

profile of v5, /device:TPU:0, one launch (start us, length us, event | category | flops | bytes accessed | tf_op | source)
XLA Modules:
  0.0 136.4 jit_solution(10610358125147490223)
XLA Ops:
  0.0 134.7 %layer.1 = bf16[32,4096]{1,0:T(8,128)(2,1)} custom-call(bf16[32,4096]{1,0:T(8,128)(2,1)} %refs_0_.1, f32[1,4096]{1,0:T(1,128)} %bitcast.4, bf16[64,4096]{1,0:T(8,128)(2,1)} %bitcast.3, bf16[8,128,2048]{2,1,0:T(8,128)(2,1)} %refs_3_.1, bf16[8,2048,128]{2,1,0:T(8,128)(2,1)} %refs_4_.1, s32[2,8]{1,0:T(2,128)} %refs_5_.1, bf16[64,4096]{1,0:T(8,128)(2,1)} %refs_6_.1, ...), custom_call_target="tpu_custom_call" | custom-call | tf_op jit(solution)/shard_map/layer/pallas_call | solution.py:862
  134.7 1.7 %copy.13 = bf16[32,4096]{1,0:T(8,128)(2,1)} copy(bf16[32,4096]{1,0:T(8,128)(2,1)} %layer.1) | data formatting | bytes 524288

commit v6 on v5

--- a/solution.py
+++ b/solution.py
@@ -46,6 +46,16 @@
     has = {1: a < A - 1, -1: a > 0}
     toward = {1: me + 4, -1: me - 4}
     return has, toward
+
+
+def far_first(A, a):
+    low, high = 0, A - 1
+    found = []
+    for _ in range(A):
+        left = (a - low > high - a).astype(jnp.int32)
+        found.append(high + left * (low - high))
+        low, high = low + left, high - 1 + left
+    return found
 
 
 def query_phase(
@@ -245,9 +255,10 @@
     load_kv = pltpu.make_async_copy(kv_ref, kv, local.at[1])
     load_cached.start()
     load_kv.start()
-    order = sorted(range(1, n), key=lambda s: -min(s, n - s))
-    others = [lax.rem(me + s, n) for s in order]
-    columns = [lax.rem(a + s, A) for s in range(1, A)]
+    *far, _ = far_first(A, a)
+    others = [index_of(k, bb, cc) for k in far for bb in (b, 1 - b) for cc in (c, 1 - c)]
+    others += [index_of(a, 1 - b, 1 - c), across, pair]
+    columns = far
     entering, flying = pl.ds(0, A), pl.ds(A, A)
     q_all[a, c, b] = q_ref[:A]
     q_cached[b] = q_ref[A:]
@@ -556,16 +567,6 @@
     return finish
 
 
-def far_first(A, a):
-    low, high = 0, A - 1
-    found = []
-    for _ in range(A):
-        left = (a - low > high - a).astype(jnp.int32)
-        found.append(high + left * (low - high))
-        low, high = low + left, high - 1 + left
-    return found
-
-
 def feed_phase(
     n, x_ref, gain_ref, gate_ref, up_ref, down_ref, out_ref,
     w_in, sums_in, w_down, act, part,
@@ -591,18 +592,18 @@
     scale = lax.rsqrt(jnp.mean(values * values, axis=-1, keepdims=True) + epsilon)
     for p in range(P):
         at = slice(p * W, (p + 1) * W)
-        xs[p, b, c, a] = (values[:, at] * scale * gain_ref[:, at]).astype(jnp.bfloat16)
+        xs[p, a, b, c] = (values[:, at] * scale * gain_ref[:, at]).astype(jnp.bfloat16)
 
     def z_copy(k, p, s, d):
-        block = xs.at[p, b, c, k]
+        block = xs.at[p, k, b, c]
         return remote(block, block, zs.at[(0 if d == 1 else A) + s, p], zr.at[k, p], toward[d])
 
     def y_copy(k, p, bb):
-        block = xs.at[p, bb, c, k]
+        block = xs.at[p, k, bb, c]
         return remote(block, block, ys.at[k, p], yr.at[k, p], across)
 
     def c_copy(k, p, bb, cc):
-        block = xs.at[p, bb, cc, k]
+        block = xs.at[p, k, bb, cc]
         return remote(block, block, cs.at[bb * A + k, p], cr.at[bb * A + k, p], pair)
 
     for p in range(P):
@@ -625,45 +626,88 @@
                 y_copy(k, p, 1 - b).wait_recv()
                 c_copy(k, p, 1 - b, c).start()
 
-    for s in range(1, A):
+    for sums in sums_in:
+        sums[...] = jnp.zeros_like(sums)
+    tall = 4 * rows
+
+    def hop(s, p):
+        for d in (1, -1):
+            k = a - s * d
+
+            @pl.when((k >= 0) & (k < A))
+            def _():
+                block = xs.at[p, k, b, c]
+                remote(block, block, zs.at[0, p], zr.at[k, p], toward[-d]).wait_recv()
+
+                @pl.when(has[d])
+                def _():
+                    z_copy(k, p, s, d).start()
+
+                y_copy(k, p, b).start()
+                c_copy(k, p, b, c).start()
+
+    def contract(s, p):
+        for d in (1, -1) if s else (1,):
+            k = a - s * d
+
+            @pl.when((k >= 0) & (k < A))
+            def _():
+                for bb in range(2):
+                    c_copy(k, p, bb, 1 - c).wait_recv()
+                left = xs[p, k].reshape(tall, W)
+                at = pl.ds(pl.multiple_of(k * tall, tall), tall)
+                taken = pl.ds(pl.multiple_of(p * W, W), W)
+                for w, sums in zip(w_in, sums_in):
+                    sums[at, :] += jnp.dot(left, w[taken, :], preferred_element_type=jnp.float32)
+
+    def each(visit):
+        def one(p, carry):
+            visit(p)
+            return carry
+
+        lax.fori_loop(0, P, one, 0)
+
+    each(lambda p: hop(1, p))
+    for s in range(2, A + 1):
+        if s == 3 or A < 3:
+            for load in loads:
+                load.wait()
+
+        def stage(p, s=s):
+            if s < A:
+                hop(s, p)
+            pass_on(s - 2, p)
+            if s > 2:
+                contract(s - 3, p)
+
+        each(stage)
+
+    def last(p):
+        pass_on(A - 1, p)
+        contract(A - 2, p)
+
+        @pl.when(p > 0)
+        def _():
+            contract(A - 1, p - 1)
+
+    each(last)
+    contract(A - 1, P - 1)
+
+    def activate(bb, cc):
+        found = []
+        for k in range(A):
+            at = pl.ds(pl.multiple_of((4 * k + 2 * bb + cc) * rows, rows), rows)
+            gate, up = sums_in[0][at, split[0][1]], sums_in[-1][at, split[1][1]]
+            found.append(jax.nn.gelu(gate, approximate=True) * up)
+        act[2 * bb + cc] = jnp.concatenate(found, axis=0).astype(jnp.bfloat16)
+
+    activate(1 - b, 1 - c)
+
+    def finish_gather():
         for p in range(P):
-            for d in (1, -1):
-                k = a - s * d
-
-                @pl.when((k >= 0) & (k < A))
-                def _():
-                    block = xs.at[p, b, c, k]
-                    remote(block, block, zs.at[0, p], zr.at[k, p], toward[-d]).wait_recv()
-
-                    @pl.when(has[d])
-                    def _():
-                        z_copy(k, p, s, d).start()
-
-                    y_copy(k, p, b).start()
-                    c_copy(k, p, b, c).start()
-
-            if s > 1:
-                pass_on(s - 2, p)
-    for p in range(P):
-        pass_on(A - 2, p)
-    for load in loads:
-        load.wait()
-
-    def contract(p):
-        for bb in range(2):
-            for k in range(A):
-                c_copy(k, p, bb, 1 - c).wait_recv()
-        left = xs[p].reshape(n * rows, W)
-        for w, sums in zip(w_in, sums_in):
-            found = jnp.dot(left, w[p * W : (p + 1) * W, :], preferred_element_type=jnp.float32)
-            sums[...] = found if p == 0 else sums[...] + found
-
-    for p in range(P):
-        pass_on(A - 1, p)
-        if p:
-            contract(p - 1)
-    contract(P - 1)
-    for p in range(P):
+            gathered_sends(p)
+
+    def gathered_sends(p):
         for s in range(A):
             for d in (1, -1):
                 k = a - s * d
@@ -676,12 +720,6 @@
             y_copy(k, p, b).wait_send()
             for bb in range(2):
                 c_copy(k, p, bb, c).wait_send()
-
-    tall = A * rows
-    for group in range(4):
-        at = slice(group * tall, (group + 1) * tall)
-        gate, up = sums_in[0][at, split[0][1]], sums_in[-1][at, split[1][1]]
-        act[group] = (jax.nn.gelu(gate, approximate=True) * up).astype(jnp.bfloat16)
 
     def multiply(i, p, bb, cc):
         found = jnp.dot(act[2 * bb + cc], w_down[:, p * W : (p + 1) * W], preferred_element_type=jnp.float32)
@@ -710,6 +748,7 @@
                 if p == 0:
                     multiply(0, p, 1 - b, 1 - c)
                     g_copy(0, p).start()
+                    activate(1 - b, c)
                     multiply(1, p, 1 - b, c)
                 if p + 1 < P:
                     multiply(0, p + 1, 1 - b, 1 - c)
@@ -719,6 +758,8 @@
             h_copy(k, p).start()
             if t == 0 and p + 1 < P:
                 multiply(1, p + 1, 1 - b, c)
+    activate(b, 1 - c)
+    activate(b, c)
     for p in range(P):
         multiply(2, p, b, 1 - c)
         g_copy(1, p).start()
@@ -753,6 +794,7 @@
                 at = slice(p * W, (p + 1) * W)
                 out_ref[:, at] = (x_ref[:, at].astype(jnp.float32) + part[3, p, k]).astype(jnp.bfloat16)
 
+    finish_gather()
     for t, k in enumerate(order):
         right = (k > a).astype(jnp.int32)
         for p in range(P):
@@ -853,7 +895,7 @@
     out = [VM((7, M, rows, PAD), half), VM((8, M, rows, PAD), half)] + [VM(half_piece, half)] * 3
     out += [DMA((7,)), DMA((7,)), DMA((M, P)), DMA((2 * M, P))]
     give = [
-        VM((P, 2, 2, A, rows, W), half), VM((2,) + piece, full),
+        VM((P, A, 2, 2, rows, W), half), VM((2,) + piece, full),
         VM(piece, half), VM(piece, half), VM(piece, half), VM((2,) + piece, half),
         DMA((3,)), DMA((2 * A, P)), DMA((A, P)), DMA((A, P)), DMA((A, P)), DMA((2 * A, P)), DMA((2 * A, P)),
         DMA((2, P)), DMA((2, P)), DMA((A, P)), DMA((A, P)), DMA((A, P)), DMA((2, A, P)),

time: 137 us -> 133 us (0.971)
  Pallas kernels: 135 us -> 132 us
    pallas_call x1, Pallas kernels: 135 us -> 132 us  [layer(): pl.pallas_call(functools.partial(layer_kernel, n, groups, tuple((len(part...]
where the time goes in v6:
time: 133 us
  Pallas kernels  132 us (99%)
  local copies, waits for them, and re-layouts  1.67 us (1%)
    pallas_call x1, Pallas kernels, layer(): pl.pallas_call(functools.partial(layer_kernel, n, groups, tuple((len(part...  132 us

profile of v6, /device:TPU:0, one launch (start us, length us, event | category | flops | bytes accessed | tf_op | source)
XLA Modules:
  0.0 133.3 jit_solution(2160079231018282296)
XLA Ops:
  0.0 131.6 %layer.1 = bf16[32,4096]{1,0:T(8,128)(2,1)} custom-call(bf16[32,4096]{1,0:T(8,128)(2,1)} %refs_0_.1, f32[1,4096]{1,0:T(1,128)} %bitcast.4, bf16[64,4096]{1,0:T(8,128)(2,1)} %bitcast.3, bf16[8,128,2048]{2,1,0:T(8,128)(2,1)} %refs_3_.1, bf16[8,2048,128]{2,1,0:T(8,128)(2,1)} %refs_4_.1, s32[2,8]{1,0:T(2,128)} %refs_5_.1, bf16[64,4096]{1,0:T(8,128)(2,1)} %refs_6_.1, ...), custom_call_target="tpu_custom_call" | custom-call | tf_op jit(solution)/shard_map/layer/pallas_call | solution.py:904
  131.6 1.7 %copy.13 = bf16[32,4096]{1,0:T(8,128)(2,1)} copy(bf16[32,4096]{1,0:T(8,128)(2,1)} %layer.1) | data formatting | bytes 524288

commit v7 on v6

--- a/solution.py
+++ b/solution.py
@@ -278,10 +278,11 @@
     def cached_copy(bb):
         return remote(q_ref.at[flying], q_cached.at[bb], qys.at[A], qyr.at[A], across)
 
-    def o_copy(other, spot, step):
-        at = pl.ds(pl.multiple_of(step * QLEN, QLEN), QLEN)
+    def o_copy(other, spot, column):
+        tall = pairs // 2 * QLEN
+        at = pl.ds(pl.multiple_of(column * tall, tall), tall)
         return remote(
-            o_send.at[other, at], o_recv.at[spot, at], os.at[step, other], orr.at[step, spot], other
+            o_send.at[other, at], o_recv.at[spot, at], os.at[column, other], orr.at[column, spot], other
         )
 
     def st_copy(other, spot):
@@ -336,8 +337,8 @@
 
     at_position = me * positions + lax.broadcasted_iota(jnp.int32, (1, positions), 1)
 
-    def pair_step(step, carry):
-        at = pl.ds(pl.multiple_of(step * QLEN, QLEN), QLEN)
+    def pair_step(step, spot):
+        at = pl.ds(pl.multiple_of(spot * QLEN, QLEN), QLEN)
         nothing = jnp.zeros((QLEN, PAD), jnp.bfloat16)
         for i in range(2):
             for g in range(heads // 2):
@@ -382,15 +383,15 @@
             for e in range(2):
                 even, odd = (f[e * QLEN : (e + 1) * QLEN, e * PAD : (e + 1) * PAD] for f in found)
                 o_send[2 * g + e, at, :] = jnp.where(low, pltpu.roll(odd, DH, 1), even).astype(jnp.bfloat16)
-        for other in others:
-            o_copy(other, me, step).start()
-        return carry
 
     def steps(column):
         def one(i, carry):
-            return pair_step(2 * i + column, carry)
+            pair_step(2 * i + column, column * (pairs // 2) + i)
+            return carry
 
         lax.fori_loop(0, pairs // 2, one, 0)
+        for other in others:
+            o_copy(other, me, column).start()
 
     def second_column():
         qy_copy(a, 1 - b).wait_recv()
@@ -410,8 +411,7 @@
     between[1]()
     cached_copy(1 - b).wait_recv()
     load_cached.wait()
-    first, second = requests // 4, requests // 2
-    cached_requests(0, first)
+    second = requests // 4
     load_kv.wait()
     if rows == QLEN:
         arrived(b)
@@ -423,7 +423,7 @@
         arrived(1 - b)
         steps(b)
     between[2]()
-    cached_requests(first, second)
+    cached_requests(0, second)
     if rows == QLEN:
         arrived(1 - b)
     steps(1 - b)
@@ -448,9 +448,11 @@
     )
     st_recv[...] = scale / jnp.where(total > 0.0, total, 1.0)
     short = low[:8]
+    for column in range(2):
+        for other in others:
+            o_copy(other, other, column).wait_recv()
     for step in range(pairs):
-        for other in others:
-            o_copy(other, other, step).wait_recv()
+        spot = step % 2 * (pairs // 2) + step // 2
         mixed = jnp.zeros((QLEN, PAD), jnp.float32)
         for d in range(n):
             known = st_recv[d]
@@ -459,7 +461,7 @@
                 lone = g * gap + 2 * step
                 share.append(jnp.where(short, known[:, lone + 1 : lone + 2], known[:, lone : lone + 1]))
             share = jnp.concatenate(share, axis=0)
-            mixed = mixed + share * o_recv[d, step * QLEN : (step + 1) * QLEN, :].astype(jnp.float32)
+            mixed = mixed + share * o_recv[d, spot * QLEN : (spot + 1) * QLEN, :].astype(jnp.float32)
         put(2 * step, mixed)
         put(2 * step + 1, pltpu.roll(mixed, DH, 1))
 
@@ -473,8 +475,8 @@
                 qc_copy(k, bb, c).wait_send()
         for other in others:
             st_copy(other, me).wait_send()
-            for step in range(pairs):
-                o_copy(other, me, step).wait_send()
+            for column in range(2):
+                o_copy(other, me, column).wait_send()
 
     return finish
 
@@ -888,7 +890,7 @@
         VM((n, pairs * QLEN, PAD), half), VM((n, pairs * QLEN, PAD), half),
         VM((n, 8, PAD), full), VM((n, 8, PAD), full),
         DMA((2,)), DMA((A,)), DMA((A,)), DMA((A + 1,)), DMA((A + 1,)), DMA((2 * A,)), DMA((2 * A,)),
-        DMA((pairs, n)), DMA((pairs, n)), DMA((n,)), DMA((n,)),
+        DMA((2, n)), DMA((2, n)), DMA((n,)), DMA((n,)),
     ]
     M = A // 2
     half_piece = (P, M, rows, W)

time: 133 us -> 132 us (level)
  Pallas kernels: 132 us -> 130 us
    pallas_call x1, Pallas kernels: 132 us -> 130 us  [layer(): pl.pallas_call(functools.partial(layer_kernel, n, groups, tuple((len(part...]
where the time goes in v7:
time: 132 us
  Pallas kernels  130 us (98%)
  local copies, waits for them, and re-layouts  1.67 us (1%)
    pallas_call x1, Pallas kernels, layer(): pl.pallas_call(functools.partial(layer_kernel, n, groups, tuple((len(part...  130 us

profile of v7, /device:TPU:0, one launch (start us, length us, event | category | flops | bytes accessed | tf_op | source)
XLA Modules:
  0.0 131.8 jit_solution(9644924355265038126)
XLA Ops:
  0.0 130.2 %layer.1 = bf16[32,4096]{1,0:T(8,128)(2,1)} custom-call(bf16[32,4096]{1,0:T(8,128)(2,1)} %refs_0_.1, f32[1,4096]{1,0:T(1,128)} %bitcast.4, bf16[64,4096]{1,0:T(8,128)(2,1)} %bitcast.3, bf16[8,128,2048]{2,1,0:T(8,128)(2,1)} %refs_3_.1, bf16[8,2048,128]{2,1,0:T(8,128)(2,1)} %refs_4_.1, s32[2,8]{1,0:T(2,128)} %refs_5_.1, bf16[64,4096]{1,0:T(8,128)(2,1)} %refs_6_.1, ...), custom_call_target="tpu_custom_call" | custom-call | tf_op jit(solution)/shard_map/layer/pallas_call | solution.py:906
  130.2 1.7 %copy.13 = bf16[32,4096]{1,0:T(8,128)(2,1)} copy(bf16[32,4096]{1,0:T(8,128)(2,1)} %layer.1) | data formatting | bytes 524288

commit v8 on v7

--- a/solution.py
+++ b/solution.py
@@ -144,10 +144,11 @@
 
                     c_copy(k, p, c).start()
 
-        if s < 3:
-            y_arrival(s - 1).wait_recv()
-            for twin in twins:
-                g_copy(s - 1, mine, twin).start()
+            if s in (2, 3) and p == min(1, P - 1):
+                y_arrival(s - 2).wait_recv()
+                for twin in twins:
+                    g_copy(s - 2, mine, twin).start()
+
     for twin in twins:
         g_copy(0, twin, mine).wait_recv()
     load_w.wait()
@@ -866,7 +867,7 @@
     rows, width = hidden.shape
     requests, positions, across = entering_kv.shape
     pairs, heads = requests // 2, across // PAD
-    assert A > 2 and A % 2 == 0 and DH % groups == 0 and pairs % 2 == 0
+    assert A > 3 and A % 2 == 0 and DH % groups == 0 and pairs % 2 == 0
     assert heads == n and QLEN % rows == 0 and 8 * requests <= PAD
     P = pieces_of(n, width)
     W = width // P

time: 132 us -> 131 us (level)
    pallas_call x1, Pallas kernels: 130 us -> 129 us  [layer(): pl.pallas_call(functools.partial(layer_kernel, n, groups, tuple((len(part...]
where the time goes in v8:
time: 131 us; the launch traced here: 130 us
  Pallas kernels  129 us (98%)
  local copies, waits for them, and re-layouts  1.67 us (1%)
    pallas_call x1, Pallas kernels, layer(): pl.pallas_call(functools.partial(layer_kernel, n, groups, tuple((len(part...  129 us

profile of v8, /device:TPU:0, one launch (start us, length us, event | category | flops | bytes accessed | tf_op | source)
XLA Modules:
  0.0 130.5 jit_solution(3321958194785915951)
XLA Ops:
  0.0 128.8 %layer.1 = bf16[32,4096]{1,0:T(8,128)(2,1)} custom-call(bf16[32,4096]{1,0:T(8,128)(2,1)} %refs_0_.1, f32[1,4096]{1,0:T(1,128)} %bitcast.4, bf16[64,4096]{1,0:T(8,128)(2,1)} %bitcast.3, bf16[8,128,2048]{2,1,0:T(8,128)(2,1)} %refs_3_.1, bf16[8,2048,128]{2,1,0:T(8,128)(2,1)} %refs_4_.1, s32[2,8]{1,0:T(2,128)} %refs_5_.1, bf16[64,4096]{1,0:T(8,128)(2,1)} %refs_6_.1, ...), custom_call_target="tpu_custom_call" | custom-call | tf_op jit(solution)/shard_map/layer/pallas_call | solution.py:907
  128.8 1.7 %copy.13 = bf16[32,4096]{1,0:T(8,128)(2,1)} copy(bf16[32,4096]{1,0:T(8,128)(2,1)} %layer.1) | data formatting | bytes 524288
